TPU v7x, 128 devices: a whole 4x4x4 slice. The times are simulated.
128 devices in a mesh: dev: 128 (over x, z, y, core).
Axes of the slice: x: 4, y: 4, z: 4, core: 2. Of those that a mesh axis runs over, the one named last changes fastest.
Arguments:
- pixels: float32 [4, 2048, 8192], P(None, 'dev'), may hold values from -10 to 10
- valid_flags: int32 [4, 2048, 8192], P(None, 'dev'), may hold values 0 or 1
Outputs:
- tile_halves: float32 [128, 256, 2048], P('dev')
- header: float32 [5, 4], replicated
All inputs are finite; a program needn't handle non-finite values. No bound on the sum of `valid_flags` on one device may be relied on, other than what follows from the above.
Results may differ from a plain program's by a relative error of at most 0.00002.
Values sent between devices are 32-bit elements; how exact they have to be, the bound alone decides.
A program may use at most 128 MiB of HBM per device.

v0:
```python
import jax
import jax.numpy as jnp
from jax import lax
from jax.sharding import Mesh
from jax.sharding import PartitionSpec as P

TILE = 512
DEV = ("dev_0", "dev_1", "dev_2", "dev_3")


largest_value = 3e38


def from_partner(value, axis, stride):
    mask = 2**stride
    pairs = [(source, source ^ mask) for source in range(lax.axis_size(axis))]
    return lax.ppermute(value, axis, pairs)


def gathered_once(x, axis):
    leaves = jax.tree.leaves(x)
    sequence = sorted(range(len(leaves)), key=lambda k: -leaves[k].size)
    width = (1, *leaves[sequence[0]].shape)[-1]
    lines = [
        jnp.pad(leaves[k].reshape(-1), (0, -leaves[k].size % width)).reshape(-1, width)
        for k in sequence
    ]
    both, at, found = (lax.all_gather(jnp.concatenate(lines), axis), 0, {})
    for k, line in zip(sequence, lines):
        section = both[:, at : at + len(line)].reshape(len(both), -1)
        found[k] = section[:, : leaves[k].size].reshape(-1, *leaves[k].shape)
        at += len(line)
    numbers = iter(range(len(leaves)))
    return jax.tree.map(lambda _: found[next(numbers)], x)


def merged_by_axis(x, axes, combine):
    for axis in axes:
        pieces = gathered_once(x, axis)
        x = jax.tree.map(lambda part: part[0], pieces)
        for k in range(1, lax.axis_size(axis)):
            x = combine(x, jax.tree.map(lambda part: part[k], pieces))
    return x


def combine_centred(earlier, later):
    merged_count = earlier[2] + later[2]
    mean_gap = later[3] - earlier[3]
    weight = later[2] / jnp.maximum(merged_count, 1.0)
    return (
        jnp.minimum(earlier[0], later[0]),
        jnp.maximum(earlier[1], later[1]),
        merged_count,
        earlier[3] + mean_gap * weight,
        earlier[4] + later[4] + mean_gap * mean_gap * earlier[2] * weight,
    )


def section_split(result, position, bit_index, members):
    own_bit = position >> bit_index & 1
    paired = result.reshape((members >> bit_index + 1, 2, 1 << bit_index) + result.shape[1:])
    lower_half = paired[:, 0]
    upper_half = paired[:, 1]
    outgoing = jnp.where(own_bit == 1, lower_half, upper_half)
    return (own_bit, lower_half, upper_half, outgoing)


def section_join(result, own_bit, lower_half, upper_half, incoming):
    new_lower = jnp.where(own_bit == 1, incoming, lower_half)
    new_upper = jnp.where(own_bit == 1, upper_half, incoming)
    return jnp.stack([new_lower, new_upper], axis=1).reshape(result.shape)


def on_device(pixels, valid_flags):
    band_total, strip_rows, columns = pixels.shape
    members = columns // TILE
    usable = valid_flags == 1
    filled = jnp.where(usable, pixels, jnp.float32(0.0))
    pieces = jnp.transpose(filled.reshape(band_total, strip_rows, members, TILE), (2, 1, 3, 0))
    pieces = pieces.reshape(members, strip_rows, TILE * band_total)
    position = lax.axis_index(DEV) % members
    section_count = members.bit_length() - 1
    result = pieces
    for bit_index in range(section_count):
        own_bit, lower_half, upper_half, outgoing = section_split(
            result, position, bit_index, members
        )
        incoming = from_partner(outgoing, DEV, bit_index)
        result = section_join(result, own_bit, lower_half, upper_half, incoming)
    tile_halves = result.reshape(1, members * strip_rows, TILE * band_total)
    lowest = jnp.min(jnp.where(usable, pixels, jnp.float32(largest_value)), axis=(1, 2))
    highest = jnp.max(jnp.where(usable, pixels, jnp.float32(-largest_value)), axis=(1, 2))
    valid_count = jnp.sum(usable.astype(jnp.float32), axis=(1, 2))
    band_sum = jnp.sum(filled, axis=(1, 2))
    local_mean = band_sum / jnp.maximum(valid_count, 1.0)
    deviation = jnp.where(usable, pixels - local_mean[:, None, None], jnp.float32(0.0))
    spread = jnp.sum(deviation * deviation, axis=(1, 2))
    merged = merged_by_axis(
        (lowest, highest, valid_count, local_mean, spread), DEV, combine_centred
    )
    average = merged[3]
    variance = merged[4] / jnp.maximum(merged[2], 1.0)
    cell_total = strip_rows * columns * lax.axis_size(DEV)
    header = jnp.stack(
        [
            merged[0],
            merged[1],
            merged[2] / cell_total,
            average,
            jnp.sqrt(jnp.maximum(variance, 0.25)),
        ]
    )
    return (tile_halves, header)


def solution(mesh):
    split = Mesh(mesh.devices.reshape(4, 4, 4, 2), ("dev_0", "dev_1", "dev_2", "dev_3"))
    placed = (P(None, DEV, None), P(None, DEV, None))
    return jax.shard_map(
        on_device, mesh=split, in_specs=placed, out_specs=(P(DEV, None, None), P()), check_vma=False
    )
```

profile of v0, /device:TPU:6, one launch (start us, length us, event | category | flops | bytes accessed | tf_op | source)
XLA Modules:
  0.0 147.8 jit_solution(4155668410068421382)
XLA Ops:
  0.6 2.2 %convert_reduce_fusion = (f32[4]{0:T(128)S(1)}, pred[4,16,8192]{2,1,0:T(8,128)(4,1)S(1)}) fusion(s32[4,16,8192]{2,1,0:T(8,128)} %param.3), kind=kLoop, calls=%fused_computation.11 | loop fusion | flops 1572860 | bytes 2621456 | tf_op jit(solution)/shard_map/reduce_sum | solution.py:93
  2.8 2.0 %fusion.31 = (f32[4]{0:T(128)S(1)}, f32[4,16,8192]{2,1,0:T(8,128)S(1)}) fusion(pred[4,16,8192]{2,1,0:T(8,128)(4,1)S(1)} %get-tuple-element.57, f32[4,16,8192]{2,1,0:T(8,128)} %param.2), kind=kLoop, calls=%fused_computation.172 | loop fusion | flops 1048572 | bytes 4718608 | tf_op jit(solution)/shard_map/reduce_sum | solution.py:94
  4.8 10.7 %copy.51 = f32[4,16,8192]{1,0,2:T(4,128)} copy(f32[4,16,8192]{2,1,0:T(8,128)S(1)} %get-tuple-element.59) | data formatting | bytes 4194304 | tf_op jit(solution)/shard_map/reshape | solution.py:79
  15.5 9.8 %fusion.1 = f32[8,1,16,2048]{2,3,0,1:T(8,128)} fusion(f32[8,2,1,16,2048]{3,4,1,0,2:T(8,128)} %bitcast.544, pred[]{:T(512)S(6)} %eq.31), kind=kLoop, calls=%fused_computation.3 | loop fusion | flops 262144 | bytes 3145729 | tf_op jit(solution)/shard_map/jit(_where)/select_n | solution.py:64
  25.4 5.1 %copy.37 = f32[8,1,16,2048]{3,2,1,0:T(8,128)S(1)} copy(f32[8,1,16,2048]{2,3,0,1:T(8,128)} %fusion.1) | data formatting | bytes 2097152 | tf_op jit(solution)/shard_map/jit(_where)/select_n | solution.py:64
  30.5 0.1 collective-permute-start
  30.6 2.6 %collective-permute-done = f32[8,1,16,2048]{3,2,1,0:T(8,128)S(1)} collective-permute-done((f32[8,1,16,2048]{3,2,1,0:T(8,128)S(1)}, f32[8,1,16,2048]{3,2,1,0:T(8,128)S(1)}, u32[]{:S(2)}, u32[]{:S(2)}) %collective-permute-start) | collective-permute-done | bytes 1048608 | tf_op jit(solution)/shard_map/ppermute | solution.py:17
  33.2 4.6 %copy.38 = f32[8,1,16,2048]{2,3,0,1:T(8,128)} copy(f32[8,1,16,2048]{3,2,1,0:T(8,128)S(1)} %collective-permute-done) | data formatting | bytes 2097152 | tf_op jit(solution)/shard_map/ppermute | solution.py:17
  37.8 15.1 %fusion = (f32[8,1,16,2048]{2,3,0,1:T(8,128)}, f32[8,1,16,2048]{2,3,0,1:T(8,128)}) fusion(f32[8,1,16,2048]{2,3,0,1:T(8,128)} %copy.38, f32[8,2,1,16,2048]{3,4,1,0,2:T(8,128)} %bitcast.545, pred[]{:T(512)S(6)} %eq.31), kind=kLoop, calls=%fused_computation.2 | loop fusion | flops 524288 | bytes 5242881 | tf_op jit(solution)/shard_map/jit(_where)/select_n | solution.py:69
  52.9 5.1 %copy.39 = f32[8,1,16,2048]{3,2,0,1:T(8,128)S(1)} copy(f32[8,1,16,2048]{2,3,0,1:T(8,128)} %get-tuple-element.60) | data formatting | bytes 2097152 | tf_op jit(solution)/shard_map/jit(_where)/select_n | solution.py:69
  58.0 5.1 %copy.41 = f32[8,1,16,2048]{3,2,0,1:T(8,128)S(1)} copy(f32[8,1,16,2048]{2,3,0,1:T(8,128)} %get-tuple-element.61) | data formatting | bytes 2097152 | tf_op jit(solution)/shard_map/jit(_where)/select_n | solution.py:70
  63.1 1.1 broadcast_select_fusion.1
  64.2 1.6 %collective-permute-start.1 = (f32[4,2,16,2048]{3,2,0,1:T(8,128)}, f32[4,2,16,2048]{3,2,0,1:T(8,128)}, u32[]{:S(2)}, u32[]{:S(2)}) collective-permute-start(f32[4,2,16,2048]{3,2,0,1:T(8,128)} %broadcast_select_fusion.1), channel_id=1, source_target_pairs={{0,2},{1,3},{2,0},{3,1},{4,6},{5,7},{6,4},{7,5},{8,10},{9,11},{10,... | collective-permute-start | bytes 3145736 | tf_op jit(solution)/shard_map/ppermute | solution.py:17
  65.8 23.9 %collective-permute-done.1 = f32[4,2,16,2048]{3,2,0,1:T(8,128)} collective-permute-done((f32[4,2,16,2048]{3,2,0,1:T(8,128)}, f32[4,2,16,2048]{3,2,0,1:T(8,128)}, u32[]{:S(2)}, u32[]{:S(2)}) %collective-permute-start.1) | collective-permute-done | bytes 1048608 | tf_op jit(solution)/shard_map/ppermute | solution.py:17
  89.7 1.4 select_bitcast_fusion.5
  91.1 0.1 pad_maximum_fusion
  91.3 0.1 copy.43
  91.4 0.0 copy-start.1
  91.4 0.0 copy-start
  91.4 1.1 fusion.6
  92.6 3.2 %collective-permute-start.2 = (f32[2,4,16,2048]{3,2,1,0:T(8,128)}, f32[2,4,16,2048]{3,2,1,0:T(8,128)}, u32[]{:S(2)}, u32[]{:S(2)}) collective-permute-start(f32[2,4,16,2048]{3,2,1,0:T(8,128)} %fusion.6), channel_id=1, source_target_pairs={{0,4},{1,5},{2,6},{3,7},{4,0},{5,1},{6,2},{7,3},{8,12},{9,13},{10,... | collective-permute-start | bytes 3145736 | tf_op jit(solution)/shard_map/ppermute | solution.py:17
  95.8 0.0 copy-done
  95.8 1.3 multiply_reduce_fusion
  97.2 0.1 copy.46
  97.3 10.2 %all-gather.4 = f32[4,5,4]{1,2,0:T(4,128)S(1)} all-gather(f32[1,5,4]{1,2,0:T(4,128)S(1)} %bitcast.558), channel_id=2, replica_groups=mesh['dev_0'=4,'dev_1'=4,'dev_2'=4,'dev_3'=2] {'dev_0'}, dimensions={0}, use_global_device_ids=true | all-gather | bytes 400 | tf_op jit(solution)/shard_map/all_gather | solution.py:28
  107.4 0.2 slice_reduce_fusion.24
  107.6 0.4 fusion.17
  108.1 0.1 copy.47
  108.2 12.0 %all-gather.5 = f32[4,5,4]{1,2,0:T(4,128)S(1)} all-gather(f32[1,5,4]{1,2,0:T(4,128)S(1)} %bitcast.557), channel_id=3, replica_groups=mesh['dev_0'=4,'dev_1'=4,'dev_2'=4,'dev_3'=2] {'dev_1'}, dimensions={0}, use_global_device_ids=true | all-gather | bytes 400 | tf_op jit(solution)/shard_map/all_gather | solution.py:28
  120.2 0.4 fusion.14
  120.5 0.0 collective-permute-done.2
  120.5 1.7 %select_bitcast_fusion.3 = (f32[2,1,4,16,2048]{4,3,2,0,1:T(8,128)S(1)}, f32[2,1,4,16,2048]{4,3,2,0,1:T(8,128)S(1)}) fusion(f32[2,4,16,2048]{3,2,1,0:T(8,128)} %collective-permute-done.2, pred[]{:T(512)S(6)} %eq.15, f32[2,2,4,16,2048]{4,3,2,1,0:T(8,128)} %bitcast.555, f32[2,2,4,16,2048]{4,3,1,0,2:T(8,128)S(1)} %bitcast.549), kind=kLoop, calls=%fused_computation.25 | loop fusion | flops 524288 | bytes 5242881 | tf_op jit(solution)/shard_map/stack | solution.py:71
  122.3 0.2 pad_maximum_fusion.1
  122.5 0.2 copy.45
  122.7 0.1 fusion.7
  122.9 1.7 %collective-permute-start.3 = (f32[1,8,16,2048]{3,2,1,0:T(8,128)S(1)}, f32[1,8,16,2048]{3,2,1,0:T(8,128)}, u32[]{:S(2)}, u32[]{:S(2)}) collective-permute-start(f32[1,8,16,2048]{3,2,1,0:T(8,128)S(1)} %fusion.7), channel_id=1, source_target_pairs={{0,8},{1,9},{2,10},{3,11},{4,12},{5,13},{6,14},{7,15},{8,0},{9,1},... | collective-permute-start | bytes 3145736 | tf_op jit(solution)/shard_map/ppermute | solution.py:17
  124.6 0.2 slice_reduce_fusion.14
  124.8 0.1 copy.48
  124.9 10.4 %all-gather.6 = f32[4,5,4]{1,2,0:T(4,128)S(1)} all-gather(f32[1,5,4]{1,2,0:T(4,128)S(1)} %bitcast.559), channel_id=4, replica_groups=mesh['dev_0'=4,'dev_1'=4,'dev_2'=4,'dev_3'=2] {'dev_2'}, dimensions={0}, use_global_device_ids=true | all-gather | bytes 400 | tf_op jit(solution)/shard_map/all_gather | solution.py:28
  135.3 0.2 slice_reduce_fusion.4
  135.5 0.4 fusion.11
  136.0 0.1 copy.49
  136.0 1.8 %all-gather.7 = f32[2,5,4]{1,2,0:T(4,128)S(1)} all-gather(f32[1,5,4]{1,2,0:T(4,128)S(1)} %bitcast.560), channel_id=5, replica_groups=mesh['dev_0'=4,'dev_1'=4,'dev_2'=4,'dev_3'=2] {'dev_3'}, dimensions={0}, use_global_device_ids=true | all-gather | bytes 240 | tf_op jit(solution)/shard_map/all_gather | solution.py:28
  137.9 0.3 fusion.8
  138.2 0.7 copy.50
  138.9 6.0 %collective-permute-done.3 = f32[1,8,16,2048]{3,2,1,0:T(8,128)} collective-permute-done((f32[1,8,16,2048]{3,2,1,0:T(8,128)S(1)}, f32[1,8,16,2048]{3,2,1,0:T(8,128)}, u32[]{:S(2)}, u32[]{:S(2)}) %collective-permute-start.3) | collective-permute-done | bytes 1048608 | tf_op jit(solution)/shard_map/ppermute | solution.py:17
  144.9 1.4 select_bitcast_fusion.1
  146.4 1.5 pad_maximum_fusion.2
  (12 shorter events, 0.2 us)
Async XLA Ops:
  30.5 2.7 %collective-permute-start = (f32[8,1,16,2048]{3,2,1,0:T(8,128)S(1)}, f32[8,1,16,2048]{3,2,1,0:T(8,128)S(1)}, u32[]{:S(2)}, u32[]{:S(2)}) collective-permute-start(f32[8,1,16,2048]{3,2,1,0:T(8,128)S(1)} %copy.37), channel_id=1, source_target_pairs={{0,1},{1,0},{2,3},{3,2},{4,5},{5,4},{6,7},{7,6},{8,9},{9,8},{10,11... | collective-permute-start | bytes 3145736 | tf_op jit(solution)/shard_map/ppermute | solution.py:17
  64.2 25.5 %collective-permute-start.1 = (f32[4,2,16,2048]{3,2,0,1:T(8,128)}, f32[4,2,16,2048]{3,2,0,1:T(8,128)}, u32[]{:S(2)}, u32[]{:S(2)}) collective-permute-start(f32[4,2,16,2048]{3,2,0,1:T(8,128)} %broadcast_select_fusion.1), channel_id=1, source_target_pairs={{0,2},{1,3},{2,0},{3,1},{4,6},{5,7},{6,4},{7,5},{8,10},{9,11},{10,... | collective-permute-start | bytes 3145736 | tf_op jit(solution)/shard_map/ppermute | solution.py:17
  91.4 5.7 %copy-start.1 = (f32[4,2,2,16,2048]{4,3,2,1,0:T(8,128)}, f32[4,2,2,16,2048]{4,3,2,1,0:T(8,128)S(1)}, u32[]{:S(2)}) copy-start(f32[4,2,2,16,2048]{4,3,2,1,0:T(8,128)S(1)} %copy.43) | copy-start | bytes 6291460
  91.4 4.4 %copy-start = (f32[4,16,8192]{2,1,0:T(8,128)S(1)}, f32[4,16,8192]{2,1,0:T(8,128)}, u32[]{:S(2)}) copy-start(f32[4,16,8192]{2,1,0:T(8,128)} %param.2) | copy-start | bytes 6291460
  92.6 27.9 %collective-permute-start.2 = (f32[2,4,16,2048]{3,2,1,0:T(8,128)}, f32[2,4,16,2048]{3,2,1,0:T(8,128)}, u32[]{:S(2)}, u32[]{:S(2)}) collective-permute-start(f32[2,4,16,2048]{3,2,1,0:T(8,128)} %fusion.6), channel_id=1, source_target_pairs={{0,4},{1,5},{2,6},{3,7},{4,0},{5,1},{6,2},{7,3},{8,12},{9,13},{10,... | collective-permute-start | bytes 3145736 | tf_op jit(solution)/shard_map/ppermute | solution.py:17
  122.9 22.1 %collective-permute-start.3 = (f32[1,8,16,2048]{3,2,1,0:T(8,128)S(1)}, f32[1,8,16,2048]{3,2,1,0:T(8,128)}, u32[]{:S(2)}, u32[]{:S(2)}) collective-permute-start(f32[1,8,16,2048]{3,2,1,0:T(8,128)S(1)} %fusion.7), channel_id=1, source_target_pairs={{0,8},{1,9},{2,10},{3,11},{4,12},{5,13},{6,14},{7,15},{8,0},{9,1},... | collective-permute-start | bytes 3145736 | tf_op jit(solution)/shard_map/ppermute | solution.py:17
where the time goes:
time: 148 us
  other arithmetic  40.7 us (28%)
  blocking collectives  34.5 us (23%)
  local copies, waits for them, and re-layouts  32.7 us (22%)
  waiting for transfers between devices  32.6 us (22%)
  starting transfers between devices  6.56 us (4%)
    all_gather x4, blocking collectives, gathered_once(): both, at, found = (lax.all_gather(jnp.concatenate(lines), axis), 0, {})  34.5 us
    ppermute x4, waiting for transfers between devices, from_partner(): return lax.ppermute(value, axis, pairs)  32.6 us
    select_n x1, other arithmetic, section_join(): new_lower = jnp.where(own_bit == 1, incoming, lower_half)  15.1 us
    select_n x4, other arithmetic, section_split(): outgoing = jnp.where(own_bit == 1, lower_half, upper_half)  12.2 us
    reshape x1, local copies, waits for them, and re-layouts, on_device(): filled.reshape(band_total, strip_rows, members, TILE)  10.7 us
    ppermute x4, starting transfers between devices, from_partner(): return lax.ppermute(value, axis, pairs)  6.56 us
    another operation x6, other arithmetic, section_join(): return jnp.stack([new_lower, new_upper], axis=1).reshape(result.shape)  6.38 us
    select_n x1, local copies, waits for them, and re-layouts, section_join(): new_upper = jnp.where(own_bit == 1, upper_half, incoming)  5.12 us
  transfers between devices with their start and end apart: 4, of which 3 were waited for; matrix products, arithmetic and copies ran while one was open for 3% of the time, Pallas kernels for 0%

commit v1 on v0

v1 whole, which is shorter than its diff:
```python
import jax
import jax.numpy as jnp
from jax import lax
from jax.experimental import pallas as pl
from jax.experimental.pallas import tpu as pltpu
from jax.sharding import PartitionSpec as P

BANDS = 4
TILE = 512
STRIP = 16
GROUP = 16
HALF = 256
N_DEV = 128
WIDE = TILE * BANDS
CELLS = 16777216.0
LARGEST = 3e38
LANES = 128


def partner(pos, i):
    dy = 3 - i % 4
    dc = 1 - (i // 4) % 2
    dz = 1 - i // 8
    z, y, c = pos // 8, (pos // 2) % 4, pos % 2
    return ((z + dz) % 2) * 8 + ((y + dy) % 4) * 2 + (c + dc) % 2


def far_partner(me, k):
    group, pos = me // GROUP, me % GROUP
    return ((group + k) % 8) * GROUP + pos


def merge(a, b, row):
    return jnp.where(row == 0, jnp.minimum(a, b), jnp.where(row == 1, jnp.maximum(a, b), a + b))


def kernel(px_hbm, fl_hbm, out, header, px, fl, send, stat_own, stat_in, group_own, group_in,
           in_sem, send_sem, recv_sem, s1_send, s1_recv, s2_send, s2_recv):
    me = lax.axis_index("dev")
    base = (me // GROUP) * GROUP
    pos = me % GROUP

    def load_px(i):
        at = pl.multiple_of(partner(pos, i) * TILE, TILE)
        return pltpu.make_async_copy(px_hbm.at[:, :, pl.ds(at, TILE)], px.at[i], in_sem.at[0, i])

    def load_fl(i):
        at = pl.multiple_of(partner(pos, i) * TILE, TILE)
        return pltpu.make_async_copy(fl_hbm.at[:, :, pl.ds(at, TILE)], fl.at[i], in_sem.at[1, i])

    def start_load(i, _):
        load_px(i).start()
        load_fl(i).start()
        return 0

    lax.fori_loop(0, GROUP, start_load, 0)

    barrier = pltpu.get_barrier_semaphore()

    def greet(i, _):
        pl.semaphore_signal(barrier, inc=1, device_id=(base + partner(pos, i),),
                            device_id_type=pl.DeviceIdType.MESH)
        return 0

    def greet_far(k, _):
        pl.semaphore_signal(barrier, inc=1, device_id=(far_partner(me, k),),
                            device_id_type=pl.DeviceIdType.MESH)
        return 0

    lax.fori_loop(0, 15, greet, 0)
    lax.fori_loop(1, 8, greet_far, 0)

    my_rows = pl.multiple_of(pos * STRIP, STRIP)

    def piece(i):
        return pltpu.make_async_remote_copy(
            src_ref=send.at[i], dst_ref=out.at[pl.ds(my_rows, STRIP)],
            send_sem=send_sem.at[i], recv_sem=recv_sem.at[i],
            device_id=(base + partner(pos, i),), device_id_type=pl.DeviceIdType.MESH)

    def stat_copy(i):
        return pltpu.make_async_remote_copy(
            src_ref=stat_own, dst_ref=stat_in.at[i],
            send_sem=s1_send.at[i], recv_sem=s1_recv.at[i],
            device_id=(base + partner(pos, i),), device_id_type=pl.DeviceIdType.MESH)

    def group_copy(k):
        return pltpu.make_async_remote_copy(
            src_ref=group_own, dst_ref=group_in.at[k],
            send_sem=s2_send.at[k], recv_sem=s2_recv.at[k],
            device_id=(far_partner(me, k),), device_id_type=pl.DeviceIdType.MESH)

    lane = lax.broadcasted_iota(jnp.int32, (8, LANES), 1)
    row = lax.broadcasted_iota(jnp.int32, (8, LANES), 0)
    block = lane // 32
    order = [((q + lane % 4) % 4) * 32 + lane // 4 for q in range(4)]

    def work(i, carry, store):
        load_px(i).wait()
        load_fl(i).wait()
        low, high, count, total, square = carry
        low, high, count, total, square = list(low), list(high), list(count), list(total), list(square)
        sums = [[] for _ in range(BANDS)]
        squares = [[] for _ in range(BANDS)]
        for r in range(2):
            for j in range(4):
                turned = []
                for b in range(BANDS):
                    value = px[i, b, pl.ds(8 * r, 8), pl.ds(LANES * j, LANES)]
                    flag = fl[i, b, pl.ds(8 * r, 8), pl.ds(LANES * j, LANES)]
                    usable = flag == 1
                    filled = jnp.where(usable, value, 0.0)
                    low[b] = jnp.minimum(low[b], jnp.where(usable, value, LARGEST))
                    high[b] = jnp.maximum(high[b], jnp.where(usable, value, -LARGEST))
                    count[b] = count[b] + flag
                    sums[b].append(filled)
                    squares[b].append(filled * filled)
                    turned.append(filled if b == 0 else pltpu.roll(filled, 32 * b, 1))
                for q in range(4):
                    mixed = turned[(0 - q) % 4]
                    for k in range(1, 4):
                        mixed = jnp.where(block == k, turned[(k - q) % 4], mixed)
                    store(r, j * 4 + q, jnp.take_along_axis(mixed, order[q], axis=1))

        def tree(parts):
            while len(parts) > 1:
                parts = [a + b for a, b in zip(parts[::2], parts[1::2])]
            return parts[0]

        for b in range(BANDS):
            total[b] = total[b] + tree(sums[b])
            square[b] = square[b] + tree(squares[b])
        return (tuple(low), tuple(high), tuple(count), tuple(total), tuple(square))

    zero = jnp.zeros((8, LANES), jnp.float32)
    carry = (
        (zero + LARGEST,) * BANDS, (zero - LARGEST,) * BANDS,
        (jnp.zeros((8, LANES), jnp.int32),) * BANDS, (zero,) * BANDS, (zero,) * BANDS,
    )

    def step(i, carry):
        def store(r, c, value):
            send[i, pl.ds(8 * r, 8), pl.ds(LANES * c, LANES)] = value

        carry = work(i, carry, store)

        @pl.when(i == 0)
        def _():
            pl.semaphore_wait(barrier, 22)

        piece(i).start()
        return carry

    carry = lax.fori_loop(0, 15, step, carry)

    def store_own(r, c, value):
        out[pl.ds(pl.multiple_of(my_rows + 8 * r, 8), 8), pl.ds(LANES * c, LANES)] = value

    low, high, count, total, square = work(15, carry, store_own)

    stats = jnp.zeros((8, LANES), jnp.float32)
    for b in range(BANDS):
        for s, value in enumerate((
            jnp.min(low[b], axis=(0, 1), keepdims=True),
            jnp.max(high[b], axis=(0, 1), keepdims=True),
            jnp.sum(count[b].astype(jnp.float32), axis=(0, 1), keepdims=True),
            jnp.sum(total[b], axis=(0, 1), keepdims=True),
            jnp.sum(square[b], axis=(0, 1), keepdims=True),
        )):
            stats = jnp.where((row == s) & (lane == b), value, stats)
    stat_own[...] = stats

    def start_stat(i, _):
        stat_copy(i).start()
        return 0

    lax.fori_loop(0, 15, start_stat, 0)

    def take_stat(i, acc):
        stat_copy(i).wait_recv()
        return merge(acc, stat_in[i], row)

    acc = lax.fori_loop(0, 15, take_stat, stat_own[...])
    group_own[...] = acc

    def start_group(k, _):
        group_copy(k).start()
        return 0

    lax.fori_loop(1, 8, start_group, 0)

    def take_group(k, acc):
        group_copy(k).wait_recv()
        return merge(acc, group_in[k], row)

    acc = lax.fori_loop(1, 8, take_group, acc)
    valid = acc[2:3]
    divisor = jnp.maximum(valid, 1.0)
    average = acc[3:4] / divisor
    variance = acc[4:5] / divisor - average * average
    header[0:1, :] = acc[0:1, :BANDS]
    header[1:2, :] = acc[1:2, :BANDS]
    header[2:3, :] = (valid / CELLS)[:, :BANDS]
    header[3:4, :] = average[:, :BANDS]
    header[4:5, :] = jnp.sqrt(jnp.maximum(variance, 0.25))[:, :BANDS]

    def finish(i, _):
        piece(i).wait_send()
        piece(i).wait_recv()
        stat_copy(i).wait_send()
        return 0

    lax.fori_loop(0, 15, finish, 0)

    def finish_far(k, _):
        group_copy(k).wait_send()
        return 0

    lax.fori_loop(1, 8, finish_far, 0)


def on_device(pixels, valid_flags):
    dma = pltpu.SemaphoreType.DMA
    tile, header = pl.pallas_call(
        kernel,
        out_shape=(
            jax.ShapeDtypeStruct((HALF, WIDE), jnp.float32),
            jax.ShapeDtypeStruct((5, BANDS), jnp.float32),
        ),
        in_specs=[pl.BlockSpec(memory_space=pl.ANY)] * 2,
        out_specs=(pl.BlockSpec(memory_space=pltpu.VMEM), pl.BlockSpec(memory_space=pltpu.VMEM)),
        scratch_shapes=[
            pltpu.VMEM((GROUP, BANDS, STRIP, TILE), jnp.float32),
            pltpu.VMEM((GROUP, BANDS, STRIP, TILE), jnp.int32),
            pltpu.VMEM((GROUP - 1, STRIP, WIDE), jnp.float32),
            pltpu.VMEM((8, LANES), jnp.float32),
            pltpu.VMEM((GROUP - 1, 8, LANES), jnp.float32),
            pltpu.VMEM((8, LANES), jnp.float32),
            pltpu.VMEM((8, 8, LANES), jnp.float32),
            dma((2, GROUP)), dma((GROUP - 1,)), dma((GROUP - 1,)),
            dma((GROUP - 1,)), dma((GROUP - 1,)), dma((8,)), dma((8,)),
        ],
        compiler_params=pltpu.CompilerParams(collective_id=0, has_side_effects=True),
        name="export",
    )(pixels, valid_flags)
    return tile.reshape(1, HALF, WIDE), header


def solution(mesh):
    placed = (P(None, "dev", None), P(None, "dev", None))
    return jax.shard_map(
        on_device, mesh=mesh, in_specs=placed, out_specs=(P("dev", None, None), P()), check_vma=False
    )
```

time: 148 us -> 51.2 us (0.35)
  the two profiles are of different devices: /device:TPU:6 before, /device:TPU:1 now
where the time goes in v1:
time: 51.2 us; the launch traced here: 51 us
  Pallas kernels  45.9 us (90%)
  local copies, waits for them, and re-layouts  4.47 us (9%)
  between operations  0.64 us (1%)
    pallas_call x1, Pallas kernels, on_device(): pl.pallas_call(kernel, out_shape=(jax.ShapeDtypeStruct((HALF, WIDE), jnp....  45.9 us
    unnamed x2, local copies, waits for them, and re-layouts  4.47 us

profile of v1, /device:TPU:1, one launch (start us, length us, event | category | flops | bytes accessed | tf_op | source)
XLA Modules:
  0.0 51.0 jit_solution(9721107538579722165)
XLA Ops:
  0.6 45.9 %export.1 = (f32[256,2048]{1,0:T(8,128)}, f32[5,4]{1,0:T(8,128)}) custom-call(f32[4,16,8192]{2,1,0:T(8,128)} %px_hbm.1, s32[4,16,8192]{2,1,0:T(8,128)} %fl_hbm.1), custom_call_target="tpu_custom_call" | custom-call | tf_op jit(solution)/shard_map/export/pallas_call | solution.py:224
  46.5 1.3 %copy.4 = f32[5,4]{0,1:T(4,128)} copy(f32[5,4]{1,0:T(8,128)} %get-tuple-element.7) | data formatting | bytes 160
  47.9 3.1 %copy.6 = f32[1,256,2048]{2,1,0:T(8,128)} copy(f32[1,256,2048]{2,1,0:T(8,128)} %bitcast.1) | data formatting | bytes 4194304

commit v2 on v1

--- a/solution.py
+++ b/solution.py
@@ -15,12 +15,20 @@
 CELLS = 16777216.0
 LARGEST = 3e38
 LANES = 128
+EARLY = 10
+
+
+STEPS = (
+    (1, 0, 0), (0, 2, 0), (1, 0, 1), (0, 2, 1), (1, 1, 0), (0, 3, 0), (1, 3, 0), (0, 1, 0),
+    (1, 1, 1), (0, 3, 1), (1, 3, 1), (0, 1, 1), (1, 2, 0), (1, 2, 1), (0, 0, 1), (0, 0, 0),
+)
+CODES = [sum((z * 8 + y * 2 + c) << (4 * k) for k, (z, y, c) in enumerate(STEPS[at:at + 7])) for at in (0, 7, 14)]
 
 
 def partner(pos, i):
-    dy = 3 - i % 4
-    dc = 1 - (i // 4) % 2
-    dz = 1 - i // 8
+    code = jnp.where(i < 7, CODES[0], jnp.where(i < 14, CODES[1], CODES[2]))
+    code = (code >> (4 * (i % 7))) % 16
+    dz, dy, dc = code // 8, (code // 2) % 4, code % 2
     z, y, c = pos // 8, (pos // 2) % 4, pos % 2
     return ((z + dz) % 2) * 8 + ((y + dy) % 4) * 2 + (c + dc) % 2
 
@@ -30,8 +38,8 @@
     return ((group + k) % 8) * GROUP + pos
 
 
-def merge(a, b, row):
-    return jnp.where(row == 0, jnp.minimum(a, b), jnp.where(row == 1, jnp.maximum(a, b), a + b))
+def merge(a, b, lane):
+    return jnp.where(lane == 0, jnp.minimum(a, b), jnp.where(lane == 1, jnp.maximum(a, b), a + b))
 
 
 def kernel(px_hbm, fl_hbm, out, header, px, fl, send, stat_own, stat_in, group_own, group_in,
@@ -148,7 +156,10 @@
         def _():
             pl.semaphore_wait(barrier, 22)
 
-        piece(i).start()
+        @pl.when(i < EARLY)
+        def _():
+            piece(i).start()
+
         return carry
 
     carry = lax.fori_loop(0, 15, step, carry)
@@ -167,7 +178,7 @@
             jnp.sum(total[b], axis=(0, 1), keepdims=True),
             jnp.sum(square[b], axis=(0, 1), keepdims=True),
         )):
-            stats = jnp.where((row == s) & (lane == b), value, stats)
+            stats = jnp.where((row == b) & (lane == s), value, stats)
     stat_own[...] = stats
 
     def start_stat(i, _):
@@ -176,9 +187,15 @@
 
     lax.fori_loop(0, 15, start_stat, 0)
 
+    def start_late(i, _):
+        piece(i).start()
+        return 0
+
+    lax.fori_loop(EARLY, 15, start_late, 0)
+
     def take_stat(i, acc):
         stat_copy(i).wait_recv()
-        return merge(acc, stat_in[i], row)
+        return merge(acc, stat_in[i], lane)
 
     acc = lax.fori_loop(0, 15, take_stat, stat_own[...])
     group_own[...] = acc
@@ -191,18 +208,17 @@
 
     def take_group(k, acc):
         group_copy(k).wait_recv()
-        return merge(acc, group_in[k], row)
+        return merge(acc, group_in[k], lane)
 
     acc = lax.fori_loop(1, 8, take_group, acc)
-    valid = acc[2:3]
+    low, high, valid = acc[:, 0:1], acc[:, 1:2], acc[:, 2:3]
     divisor = jnp.maximum(valid, 1.0)
-    average = acc[3:4] / divisor
-    variance = acc[4:5] / divisor - average * average
-    header[0:1, :] = acc[0:1, :BANDS]
-    header[1:2, :] = acc[1:2, :BANDS]
-    header[2:3, :] = (valid / CELLS)[:, :BANDS]
-    header[3:4, :] = average[:, :BANDS]
-    header[4:5, :] = jnp.sqrt(jnp.maximum(variance, 0.25))[:, :BANDS]
+    average = acc[:, 3:4] / divisor
+    variance = acc[:, 4:5] / divisor - average * average
+    deviation = jnp.sqrt(jnp.maximum(variance, 0.25))
+    table = jnp.where(lane == 0, low, jnp.where(lane == 1, high, jnp.where(
+        lane == 2, valid / CELLS, jnp.where(lane == 3, average, deviation))))
+    header[...] = table[:BANDS, :5]
 
     def finish(i, _):
         piece(i).wait_send()
@@ -225,9 +241,9 @@
         kernel,
         out_shape=(
             jax.ShapeDtypeStruct((HALF, WIDE), jnp.float32),
-            jax.ShapeDtypeStruct((5, BANDS), jnp.float32),
+            jax.ShapeDtypeStruct((BANDS, 5), jnp.float32),
         ),
-        in_specs=[pl.BlockSpec(memory_space=pl.ANY)] * 2,
+        in_specs=[pl.BlockSpec(memory_space=pltpu.HBM)] * 2,
         out_specs=(pl.BlockSpec(memory_space=pltpu.VMEM), pl.BlockSpec(memory_space=pltpu.VMEM)),
         scratch_shapes=[
             pltpu.VMEM((GROUP, BANDS, STRIP, TILE), jnp.float32),
@@ -240,10 +256,10 @@
             dma((2, GROUP)), dma((GROUP - 1,)), dma((GROUP - 1,)),
             dma((GROUP - 1,)), dma((GROUP - 1,)), dma((8,)), dma((8,)),
         ],
-        compiler_params=pltpu.CompilerParams(collective_id=0, has_side_effects=True),
+        compiler_params=pltpu.CompilerParams(collective_id=0, has_side_effects=True, vmem_limit_bytes=16 * 1024 * 1024),
         name="export",
-    )(pixels, valid_flags)
-    return tile.reshape(1, HALF, WIDE), header
+    )(pltpu.with_memory_space_constraint(pixels, pltpu.HBM), pltpu.with_memory_space_constraint(valid_flags, pltpu.HBM))
+    return tile.reshape(1, HALF, WIDE), header.T
 
 
 def solution(mesh):

time: 51.2 us -> 40.5 us (0.79)
  Pallas kernels: 45.9 us -> 37.9 us
  local copies, waits for them, and re-layouts: 4.47 us -> 1.9 us
    pallas_call x1, Pallas kernels: 45.9 us -> 37.9 us  [on_device(): pl.pallas_call(kernel, out_shape=(jax.ShapeDtypeStruct((HALF, WIDE), jnp....]
    unnamed x2, local copies, waits for them, and re-layouts: 4.47 us -> 1.9 us
where the time goes in v2:
time: 40.5 us; the launch traced here: 40.4 us
  Pallas kernels  37.9 us (94%)
  local copies, waits for them, and re-layouts  1.9 us (5%)
  between operations  0.64 us (2%)
    pallas_call x1, Pallas kernels, on_device(): pl.pallas_call(kernel, out_shape=(jax.ShapeDtypeStruct((HALF, WIDE), jnp....  37.9 us
    unnamed x2, local copies, waits for them, and re-layouts  1.9 us

profile of v2, /device:TPU:1, one launch (start us, length us, event | category | flops | bytes accessed | tf_op | source)
XLA Modules:
  0.0 40.4 jit_solution(1765940668649902987)
XLA Ops:
  0.6 37.9 %export.1 = (f32[256,2048]{1,0:T(8,128)S(1)}, f32[4,5]{1,0:T(4,128)S(1)}) custom-call(f32[4,16,8192]{2,1,0:T(8,128)} %px_hbm.1, s32[4,16,8192]{2,1,0:T(8,128)} %fl_hbm.1), custom_call_target="tpu_custom_call" | custom-call | tf_op jit(solution)/shard_map/export/pallas_call | solution.py:240
  38.5 1.3 %copy.6 = f32[1,256,2048]{2,1,0:T(8,128)} copy(f32[1,256,2048]{2,1,0:T(8,128)S(1)} %bitcast.2) | data formatting | bytes 4194304
  39.8 0.6 %copy.7 = f32[5,4]{0,1:T(4,128)} copy(f32[5,4]{0,1:T(4,128)S(1)} %bitcast.3) | data formatting | bytes 160

commit v3 on v2

--- a/solution.py
+++ b/solution.py
@@ -19,8 +19,8 @@
 
 
 STEPS = (
-    (1, 0, 0), (0, 2, 0), (1, 0, 1), (0, 2, 1), (1, 1, 0), (0, 3, 0), (1, 3, 0), (0, 1, 0),
-    (1, 1, 1), (0, 3, 1), (1, 3, 1), (0, 1, 1), (1, 2, 0), (1, 2, 1), (0, 0, 1), (0, 0, 0),
+    (1, 2, 0), (0, 2, 0), (1, 2, 1), (0, 2, 1), (1, 1, 0), (0, 3, 0), (1, 3, 0), (0, 1, 0),
+    (1, 1, 1), (0, 3, 1), (1, 3, 1), (0, 1, 1), (1, 0, 0), (1, 0, 1), (0, 0, 1), (0, 0, 0),
 )
 CODES = [sum((z * 8 + y * 2 + c) << (4 * k) for k, (z, y, c) in enumerate(STEPS[at:at + 7])) for at in (0, 7, 14)]
 
@@ -47,6 +47,7 @@
     me = lax.axis_index("dev")
     base = (me // GROUP) * GROUP
     pos = me % GROUP
+    group = me // GROUP
 
     def load_px(i):
         at = pl.multiple_of(partner(pos, i) * TILE, TILE)
@@ -71,8 +72,11 @@
         return 0
 
     def greet_far(k, _):
-        pl.semaphore_signal(barrier, inc=1, device_id=(far_partner(me, k),),
-                            device_id_type=pl.DeviceIdType.MESH)
+        @pl.when((group + k) % 8 > group)
+        def _():
+            pl.semaphore_signal(barrier, inc=1, device_id=(far_partner(me, k),),
+                                device_id_type=pl.DeviceIdType.MESH)
+
         return 0
 
     lax.fori_loop(0, 15, greet, 0)
@@ -154,7 +158,7 @@
 
         @pl.when(i == 0)
         def _():
-            pl.semaphore_wait(barrier, 22)
+            pl.semaphore_wait(barrier, 15 + group)
 
         @pl.when(i < EARLY)
         def _():
@@ -200,14 +204,35 @@
     acc = lax.fori_loop(0, 15, take_stat, stat_own[...])
     group_own[...] = acc
 
-    def start_group(k, _):
-        group_copy(k).start()
-        return 0
-
-    lax.fori_loop(1, 8, start_group, 0)
+    def to_lower(k, _):
+        @pl.when((group + k) % 8 < group)
+        def _():
+            group_copy(k).start()
+
+        return 0
+
+    lax.fori_loop(1, 8, to_lower, 0)
+
+    def to_higher(k, _):
+        @pl.when((group + 8 - k) % 8 > group)
+        def _():
+            group_copy(k).wait_recv()
+            group_copy(8 - k).start()
+
+        return 0
+
+    lax.fori_loop(1, 8, to_higher, 0)
+
+    def from_lower(k, _):
+        @pl.when((group + 8 - k) % 8 < group)
+        def _():
+            group_copy(k).wait_recv()
+
+        return 0
+
+    lax.fori_loop(1, 8, from_lower, 0)
 
     def take_group(k, acc):
-        group_copy(k).wait_recv()
         return merge(acc, group_in[k], lane)
 
     acc = lax.fori_loop(1, 8, take_group, acc)

time: 40.5 us -> 45.5 us (1.12)
  the two profiles are of different devices: /device:TPU:1 before, /device:TPU:6 now
where the time goes in v3:
time: 45.5 us; the launch traced here: 45.4 us
  Pallas kernels  42.9 us (94%)
  local copies, waits for them, and re-layouts  1.9 us (4%)
  between operations  0.64 us (1%)
    pallas_call x1, Pallas kernels, on_device(): pl.pallas_call(kernel, out_shape=(jax.ShapeDtypeStruct((HALF, WIDE), jnp....  42.9 us
    unnamed x2, local copies, waits for them, and re-layouts  1.9 us

profile of v3, /device:TPU:6, one launch (start us, length us, event | category | flops | bytes accessed | tf_op | source)
XLA Modules:
  0.0 45.4 jit_solution(8791597626583249569)
XLA Ops:
  0.6 42.9 %export.1 = (f32[256,2048]{1,0:T(8,128)S(1)}, f32[4,5]{1,0:T(4,128)S(1)}) custom-call(f32[4,16,8192]{2,1,0:T(8,128)} %px_hbm.1, s32[4,16,8192]{2,1,0:T(8,128)} %fl_hbm.1), custom_call_target="tpu_custom_call" | custom-call | tf_op jit(solution)/shard_map/export/pallas_call | solution.py:265
  43.5 1.3 %copy.6 = f32[1,256,2048]{2,1,0:T(8,128)} copy(f32[1,256,2048]{2,1,0:T(8,128)S(1)} %bitcast.2) | data formatting | bytes 4194304
  44.8 0.6 %copy.7 = f32[5,4]{0,1:T(4,128)} copy(f32[5,4]{0,1:T(4,128)S(1)} %bitcast.3) | data formatting | bytes 160

commit v4 on v2

v4 whole, which is shorter than its diff:
```python
import jax
import jax.numpy as jnp
from jax import lax
from jax.experimental import pallas as pl
from jax.experimental.pallas import tpu as pltpu
from jax.sharding import PartitionSpec as P

BANDS = 4
TILE = 512
STRIP = 16
GROUP = 16
HALF = 256
WIDE = TILE * BANDS
CELLS = 16777216.0
LARGEST = 3e38
LANES = 128
EARLY = 5
MESH = pl.DeviceIdType.MESH

STEPS = (
    (1, 2, 0), (0, 2, 0), (1, 2, 1), (0, 2, 1), (1, 1, 0), (0, 3, 0), (1, 3, 0), (0, 1, 0),
    (1, 1, 1), (0, 3, 1), (1, 3, 1), (0, 1, 1), (1, 0, 0), (1, 0, 1), (0, 0, 1), (0, 0, 0),
)
NIBBLES = [z * 8 + y * 2 + c for z, y, c in STEPS]


def packed(part):
    value = sum(code << (4 * k) for k, code in enumerate(part))
    return value - (1 << 32) if value >= 1 << 31 else value


FIRST, SECOND = packed(NIBBLES[:8]), packed(NIBBLES[8:])


def partner(pos, i):
    if isinstance(i, int):
        code = NIBBLES[i]
    else:
        code = (jnp.where(i < 8, FIRST, SECOND) >> ((i & 7) * 4)) & 15
    return ((pos ^ code) & 9) | ((pos + (code & 6)) & 6)


def far_partner(group, pos, k):
    other = ((group + 2 * (k % 4)) & 7) ^ (k // 4)
    return other, pos ^ (8 * (k // 4))


def merge(a, b, lane):
    return jnp.where(lane == 0, jnp.minimum(a, b), jnp.where(lane == 1, jnp.maximum(a, b), a + b))


def kernel(px_hbm, fl_hbm, out, header, px, fl, send, stat, total, in_sem, send_sem, recv_sem,
           s1_send, s1_recv, s2_send, s2_recv):
    me = lax.axis_index("dev")
    pos = me & 15
    group = me >> 4
    base = me - pos

    def load_px(i):
        at = pl.multiple_of(partner(pos, i) * TILE, TILE)
        return pltpu.make_async_copy(px_hbm.at[:, :, pl.ds(at, TILE)], px.at[i], in_sem.at[0, i])

    def load_fl(i):
        at = pl.multiple_of(partner(pos, i) * TILE, TILE)
        return pltpu.make_async_copy(fl_hbm.at[:, :, pl.ds(at, TILE)], fl.at[i], in_sem.at[1, i])

    for i in range(GROUP):
        load_px(i).start()
        load_fl(i).start()

    barrier = pltpu.get_barrier_semaphore()
    for i in range(15):
        pl.semaphore_signal(barrier, inc=1, device_id=(base + partner(pos, i),), device_id_type=MESH)
    for k in range(1, 8):
        other, there = far_partner(group, pos, k)

        @pl.when(other > group)
        def _():
            pl.semaphore_signal(barrier, inc=1, device_id=(other * GROUP + there,), device_id_type=MESH)

    my_rows = pl.multiple_of(pos * STRIP, STRIP)

    def piece(i):
        return pltpu.make_async_remote_copy(
            src_ref=send.at[i], dst_ref=out.at[pl.ds(my_rows, STRIP)],
            send_sem=send_sem.at[i], recv_sem=recv_sem.at[i],
            device_id=(base + partner(pos, i),), device_id_type=MESH)

    def stat_copy(i):
        return pltpu.make_async_remote_copy(
            src_ref=stat.at[pos], dst_ref=stat.at[pos],
            send_sem=s1_send.at[i], recv_sem=s1_recv.at[i],
            device_id=(base + partner(pos, i),), device_id_type=MESH)

    def total_copy(k):
        other, there = far_partner(group, pos, k)
        return pltpu.make_async_remote_copy(
            src_ref=total.at[group], dst_ref=total.at[group],
            send_sem=s2_send.at[k], recv_sem=s2_recv.at[k],
            device_id=(other * GROUP + there,), device_id_type=MESH)

    lane = lax.broadcasted_iota(jnp.int32, (8, LANES), 1)
    row = lax.broadcasted_iota(jnp.int32, (8, LANES), 0)
    block = lane // 32
    order = [((q + lane % 4) % 4) * 32 + lane // 4 for q in range(4)]

    def work(i, carry, store):
        load_px(i).wait()
        load_fl(i).wait()
        low, high, count, summed, square = [list(part) for part in carry]
        sums = [[] for _ in range(BANDS)]
        squares = [[] for _ in range(BANDS)]
        for r in range(2):
            for j in range(4):
                turned = []
                for b in range(BANDS):
                    value = px[i, b, pl.ds(8 * r, 8), pl.ds(LANES * j, LANES)]
                    flag = fl[i, b, pl.ds(8 * r, 8), pl.ds(LANES * j, LANES)]
                    usable = flag == 1
                    filled = jnp.where(usable, value, 0.0)
                    low[b] = jnp.minimum(low[b], jnp.where(usable, value, LARGEST))
                    high[b] = jnp.maximum(high[b], jnp.where(usable, value, -LARGEST))
                    count[b] = count[b] + flag
                    sums[b].append(filled)
                    squares[b].append(filled * filled)
                    turned.append(filled if b == 0 else pltpu.roll(filled, 32 * b, 1))
                for q in range(4):
                    mixed = turned[(0 - q) % 4]
                    for k in range(1, 4):
                        mixed = jnp.where(block == k, turned[(k - q) % 4], mixed)
                    store(r, j * 4 + q, jnp.take_along_axis(mixed, order[q], axis=1))

        def tree(parts):
            while len(parts) > 1:
                parts = [a + b for a, b in zip(parts[::2], parts[1::2])]
            return parts[0]

        for b in range(BANDS):
            summed[b] = summed[b] + tree(sums[b])
            square[b] = square[b] + tree(squares[b])
        return tuple(tuple(part) for part in (low, high, count, summed, square))

    zero = jnp.zeros((8, LANES), jnp.float32)
    carry = (
        (zero + LARGEST,) * BANDS, (zero - LARGEST,) * BANDS,
        (jnp.zeros((8, LANES), jnp.int32),) * BANDS, (zero,) * BANDS, (zero,) * BANDS,
    )

    def step(i, carry):
        def store(r, c, value):
            send[i, pl.ds(8 * r, 8), pl.ds(LANES * c, LANES)] = value

        carry = work(i, carry, store)

        @pl.when(i == 0)
        def _():
            pl.semaphore_wait(barrier, 15 + group)

        @pl.when(i < EARLY)
        def _():
            piece(i).start()

        return carry

    carry = lax.fori_loop(0, 15, step, carry)

    def store_own(r, c, value):
        out[pl.ds(pl.multiple_of(my_rows + 8 * r, 8), 8), pl.ds(LANES * c, LANES)] = value

    low, high, count, summed, square = work(15, carry, store_own)

    stats = zero
    for b in range(BANDS):
        for s, value in enumerate((
            jnp.min(low[b], axis=(0, 1), keepdims=True),
            jnp.max(high[b], axis=(0, 1), keepdims=True),
            jnp.sum(count[b].astype(jnp.float32), axis=(0, 1), keepdims=True),
            jnp.sum(summed[b], axis=(0, 1), keepdims=True),
            jnp.sum(square[b], axis=(0, 1), keepdims=True),
        )):
            stats = jnp.where((row == b) & (lane == s), value, stats)
    stat[pos] = stats

    for i in range(15):
        stat_copy(i).start()
    for i in range(EARLY, 15):
        piece(i).start()

    for i in range(15):
        stat_copy(i).wait_recv()
    acc = stat[0]
    for k in range(1, GROUP):
        acc = merge(acc, stat[k], lane)
    total[group] = acc

    for k in range(1, 8):
        @pl.when(far_partner(group, pos, k)[0] < group)
        def _():
            total_copy(k).start()

    back = [None, 3, 2, 1, 4, 7, 6, 5]
    for k in range(1, 8):
        @pl.when(far_partner(group, pos, back[k])[0] > group)
        def _():
            total_copy(k).wait_recv()
            total_copy(back[k]).start()

    for k in range(1, 8):
        @pl.when(far_partner(group, pos, back[k])[0] < group)
        def _():
            total_copy(k).wait_recv()

    acc = total[0]
    for k in range(1, 8):
        acc = merge(acc, total[k], lane)
    low, high, valid = acc[:, 0:1], acc[:, 1:2], acc[:, 2:3]
    divisor = jnp.maximum(valid, 1.0)
    average = acc[:, 3:4] / divisor
    variance = acc[:, 4:5] / divisor - average * average
    deviation = jnp.sqrt(jnp.maximum(variance, 0.25))
    table = jnp.where(lane == 0, low, jnp.where(lane == 1, high, jnp.where(
        lane == 2, valid / CELLS, jnp.where(lane == 3, average, deviation))))
    header[...] = table[:BANDS, :5]

    for k in range(1, 8):
        total_copy(k).wait_send()
    for i in range(15):
        stat_copy(i).wait_send()
        piece(i).wait_send()
        piece(i).wait_recv()


def on_device(pixels, valid_flags):
    dma = pltpu.SemaphoreType.DMA
    tile, header = pl.pallas_call(
        kernel,
        out_shape=(
            jax.ShapeDtypeStruct((HALF, WIDE), jnp.float32),
            jax.ShapeDtypeStruct((BANDS, 5), jnp.float32),
        ),
        in_specs=[pl.BlockSpec(memory_space=pltpu.HBM)] * 2,
        out_specs=(pl.BlockSpec(memory_space=pltpu.VMEM), pl.BlockSpec(memory_space=pltpu.VMEM)),
        scratch_shapes=[
            pltpu.VMEM((GROUP, BANDS, STRIP, TILE), jnp.float32),
            pltpu.VMEM((GROUP, BANDS, STRIP, TILE), jnp.int32),
            pltpu.VMEM((GROUP - 1, STRIP, WIDE), jnp.float32),
            pltpu.VMEM((GROUP, 8, LANES), jnp.float32),
            pltpu.VMEM((8, 8, LANES), jnp.float32),
            dma((2, GROUP)), dma((GROUP - 1,)), dma((GROUP - 1,)),
            dma((GROUP - 1,)), dma((GROUP - 1,)), dma((8,)), dma((8,)),
        ],
        compiler_params=pltpu.CompilerParams(
            collective_id=0, has_side_effects=True, vmem_limit_bytes=16 * 1024 * 1024),
        name="export",
    )(
        pltpu.with_memory_space_constraint(pixels, pltpu.HBM),
        pltpu.with_memory_space_constraint(valid_flags, pltpu.HBM),
    )
    return tile.reshape(1, HALF, WIDE), header.T


def solution(mesh):
    placed = (P(None, "dev", None), P(None, "dev", None))
    return jax.shard_map(
        on_device, mesh=mesh, in_specs=placed, out_specs=(P("dev", None, None), P()), check_vma=False
    )
```

time: 40.5 us -> 37.1 us (0.916)
  the two profiles are of different devices: /device:TPU:1 before, /device:TPU:6 now
where the time goes in v4:
time: 37.1 us; the launch traced here: 37 us
  Pallas kernels  34.4 us (93%)
  local copies, waits for them, and re-layouts  1.9 us (5%)
  between operations  0.64 us (2%)
    pallas_call x1, Pallas kernels, on_device(): pl.pallas_call(kernel, out_shape=(jax.ShapeDtypeStruct((HALF, WIDE), jnp....  34.4 us
    unnamed x2, local copies, waits for them, and re-layouts  1.9 us

profile of v4, /device:TPU:6, one launch (start us, length us, event | category | flops | bytes accessed | tf_op | source)
XLA Modules:
  0.0 37.0 jit_solution(10040170274676074749)
XLA Ops:
  0.6 34.4 %export.1 = (f32[256,2048]{1,0:T(8,128)S(1)}, f32[4,5]{1,0:T(4,128)S(1)}) custom-call(f32[4,16,8192]{2,1,0:T(8,128)} %px_hbm.1, s32[4,16,8192]{2,1,0:T(8,128)} %fl_hbm.1), custom_call_target="tpu_custom_call" | custom-call | tf_op jit(solution)/shard_map/export/pallas_call | solution.py:235
  35.1 1.3 %copy.6 = f32[1,256,2048]{2,1,0:T(8,128)} copy(f32[1,256,2048]{2,1,0:T(8,128)S(1)} %bitcast.2) | data formatting | bytes 4194304
  36.4 0.6 %copy.7 = f32[5,4]{0,1:T(4,128)} copy(f32[5,4]{0,1:T(4,128)S(1)} %bitcast.3) | data formatting | bytes 160

commit v5 on v4

--- a/solution.py
+++ b/solution.py
@@ -15,6 +15,7 @@
 LARGEST = 3e38
 LANES = 128
 EARLY = 5
+PARTS = 4
 MESH = pl.DeviceIdType.MESH
 
 STEPS = (
@@ -50,7 +51,7 @@
 
 
 def kernel(px_hbm, fl_hbm, out, header, px, fl, send, stat, total, in_sem, send_sem, recv_sem,
-           s1_send, s1_recv, s2_send, s2_recv):
+           s1_send, s1_recv, s2_send, s2_recv, ready):
     me = lax.axis_index("dev")
     pos = me & 15
     group = me >> 4
@@ -155,6 +156,12 @@
         @pl.when(i == 0)
         def _():
             pl.semaphore_wait(barrier, 15 + group)
+            for k in range(1, 8):
+                other, there = far_partner(group, pos, k)
+
+                @pl.when(other < group)
+                def _():
+                    pl.semaphore_signal(ready, inc=1, device_id=(other * GROUP + there,), device_id_type=MESH)
 
         @pl.when(i < EARLY)
         def _():
@@ -192,23 +199,14 @@
     for k in range(1, GROUP):
         acc = merge(acc, stat[k], lane)
     total[group] = acc
-
-    for k in range(1, 8):
-        @pl.when(far_partner(group, pos, k)[0] < group)
-        def _():
-            total_copy(k).start()
-
-    back = [None, 3, 2, 1, 4, 7, 6, 5]
-    for k in range(1, 8):
-        @pl.when(far_partner(group, pos, back[k])[0] > group)
-        def _():
-            total_copy(k).wait_recv()
-            total_copy(back[k]).start()
-
-    for k in range(1, 8):
-        @pl.when(far_partner(group, pos, back[k])[0] < group)
-        def _():
-            total_copy(k).wait_recv()
+    @pl.when(group < 7)
+    def _():
+        pl.semaphore_wait(ready, 7 - group)
+
+    for k in range(1, 8):
+        total_copy(k).start()
+    for k in range(1, 8):
+        total_copy(k).wait_recv()
 
     acc = total[0]
     for k in range(1, 8):
@@ -228,6 +226,18 @@
         stat_copy(i).wait_send()
         piece(i).wait_send()
         piece(i).wait_recv()
+
+
+def place(tile, header, tile_out, header_out, sems):
+    rows = HALF // PARTS
+    copies = [pltpu.make_async_copy(header, header_out, sems.at[PARTS])] + [
+        pltpu.make_async_copy(tile.at[pl.ds(rows * n, rows)], tile_out.at[pl.ds(rows * n, rows)], sems.at[n])
+        for n in range(PARTS)
+    ]
+    for copy in copies:
+        copy.start()
+    for copy in copies:
+        copy.wait()
 
 
 def on_device(pixels, valid_flags):
@@ -248,6 +258,7 @@
             pltpu.VMEM((8, 8, LANES), jnp.float32),
             dma((2, GROUP)), dma((GROUP - 1,)), dma((GROUP - 1,)),
             dma((GROUP - 1,)), dma((GROUP - 1,)), dma((8,)), dma((8,)),
+            pltpu.SemaphoreType.REGULAR,
         ],
         compiler_params=pltpu.CompilerParams(
             collective_id=0, has_side_effects=True, vmem_limit_bytes=16 * 1024 * 1024),
@@ -256,6 +267,18 @@
         pltpu.with_memory_space_constraint(pixels, pltpu.HBM),
         pltpu.with_memory_space_constraint(valid_flags, pltpu.HBM),
     )
+    tile, header = pl.pallas_call(
+        place,
+        out_shape=(
+            jax.ShapeDtypeStruct((HALF, WIDE), jnp.float32),
+            jax.ShapeDtypeStruct((BANDS, 5), jnp.float32),
+        ),
+        in_specs=[pl.BlockSpec(memory_space=pltpu.VMEM)] * 2,
+        out_specs=(pl.BlockSpec(memory_space=pltpu.HBM), pl.BlockSpec(memory_space=pltpu.HBM)),
+        scratch_shapes=[dma((PARTS + 1,))],
+        compiler_params=pltpu.CompilerParams(vmem_limit_bytes=16 * 1024 * 1024),
+        name="place",
+    )(tile, header)
     return tile.reshape(1, HALF, WIDE), header.T
 
 

time: 37.1 us -> 35.3 us (0.951)
  local copies, waits for them, and re-layouts: 1.9 us -> 0 us
    unnamed x2 -> x0, local copies, waits for them, and re-layouts: 1.9 us -> none
    pallas_call x1, Pallas kernels: 34.4 us -> 32.9 us  [on_device(): pl.pallas_call(kernel, out_shape=(jax.ShapeDtypeStruct((HALF, WIDE), jnp....]
    pallas_call x0 -> x1, Pallas kernels: none -> 1.36 us  [on_device(): pl.pallas_call(place, out_shape=(jax.ShapeDtypeStruct((HALF, WIDE), jnp.f...]
where the time goes in v5:
time: 35.3 us; the launch traced here: 34.9 us
  Pallas kernels  34.2 us (97%)
  between operations  0.64 us (2%)
    pallas_call x1, Pallas kernels, on_device(): pl.pallas_call(kernel, out_shape=(jax.ShapeDtypeStruct((HALF, WIDE), jnp....  32.9 us
    pallas_call x1, Pallas kernels, on_device(): pl.pallas_call(place, out_shape=(jax.ShapeDtypeStruct((HALF, WIDE), jnp.f...  1.36 us

profile of v5, /device:TPU:6, one launch (start us, length us, event | category | flops | bytes accessed | tf_op | source)
XLA Modules:
  0.0 34.9 jit_solution(733239985277489459)
XLA Ops:
  0.6 32.9 %export.1 = (f32[256,2048]{1,0:T(8,128)S(1)}, f32[4,5]{1,0:T(4,128)S(1)}) custom-call(f32[4,16,8192]{2,1,0:T(8,128)} %px_hbm.1, s32[4,16,8192]{2,1,0:T(8,128)} %fl_hbm.1), custom_call_target="tpu_custom_call" | custom-call | tf_op jit(solution)/shard_map/export/pallas_call | solution.py:245
  33.5 1.4 %place.1 = (f32[256,2048]{1,0:T(8,128)}, f32[4,5]{1,0:T(4,128)}) custom-call(f32[256,2048]{1,0:T(8,128)S(1)} %get-tuple-element.6.tile, f32[4,5]{1,0:T(4,128)S(1)} %get-tuple-element.7.header), custom_call_target="tpu_custom_call" | custom-call | tf_op jit(solution)/shard_map/place/pallas_call | solution.py:270

commit v6 on v5

--- a/solution.py
+++ b/solution.py
@@ -14,7 +14,8 @@
 CELLS = 16777216.0
 LARGEST = 3e38
 LANES = 128
-EARLY = 5
+EARLY = 2
+LOADS = 2
 PARTS = 4
 MESH = pl.DeviceIdType.MESH
 
@@ -33,72 +34,98 @@
 FIRST, SECOND = packed(NIBBLES[:8]), packed(NIBBLES[8:])
 
 
-def partner(pos, i):
-    if isinstance(i, int):
-        code = NIBBLES[i]
-    else:
-        code = (jnp.where(i < 8, FIRST, SECOND) >> ((i & 7) * 4)) & 15
+def moved(pos, code):
     return ((pos ^ code) & 9) | ((pos + (code & 6)) & 6)
-
-
-def far_partner(group, pos, k):
-    other = ((group + 2 * (k % 4)) & 7) ^ (k // 4)
-    return other, pos ^ (8 * (k // 4))
 
 
 def merge(a, b, lane):
     return jnp.where(lane == 0, jnp.minimum(a, b), jnp.where(lane == 1, jnp.maximum(a, b), a + b))
 
 
-def kernel(px_hbm, fl_hbm, out, header, px, fl, send, stat, total, in_sem, send_sem, recv_sem,
-           s1_send, s1_recv, s2_send, s2_recv, ready):
+def kernel(px_hbm, fl_hbm, out, header, px, fl, send, stat, part, half, in_sem, send_sem, recv_sem,
+           s1_send, s1_recv, s2_send, s2_recv, s3_send, s3_recv, ready_far):
     me = lax.axis_index("dev")
     pos = me & 15
-    group = me >> 4
     base = me - pos
+    x = me >> 5
+    high_z = (me >> 4) & 1
+    first, second = FIRST, SECOND
+
+    def target(i):
+        return moved(pos, (jnp.where(i < 8, first, second) >> ((i & 7) * 4)) & 15)
+
+    def x_partner(k):
+        return (me + 32 * k) & 127
+
+    across = me ^ 24
 
     def load_px(i):
-        at = pl.multiple_of(partner(pos, i) * TILE, TILE)
+        at = pl.multiple_of(target(i) * TILE, TILE)
         return pltpu.make_async_copy(px_hbm.at[:, :, pl.ds(at, TILE)], px.at[i], in_sem.at[0, i])
 
     def load_fl(i):
-        at = pl.multiple_of(partner(pos, i) * TILE, TILE)
+        at = pl.multiple_of(target(i) * TILE, TILE)
         return pltpu.make_async_copy(fl_hbm.at[:, :, pl.ds(at, TILE)], fl.at[i], in_sem.at[1, i])
 
-    for i in range(GROUP):
+    barrier = pltpu.get_barrier_semaphore()
+    for i in range(LOADS):
         load_px(i).start()
         load_fl(i).start()
-
-    barrier = pltpu.get_barrier_semaphore()
-    for i in range(15):
-        pl.semaphore_signal(barrier, inc=1, device_id=(base + partner(pos, i),), device_id_type=MESH)
-    for k in range(1, 8):
-        other, there = far_partner(group, pos, k)
-
-        @pl.when(other > group)
+    for code in range(1, GROUP):
+        pl.semaphore_signal(barrier, inc=1, device_id=(base + moved(pos, code),), device_id_type=MESH)
+    for k in range(1, 4):
+        @pl.when(x + k < 4)
         def _():
-            pl.semaphore_signal(barrier, inc=1, device_id=(other * GROUP + there,), device_id_type=MESH)
+            pl.semaphore_signal(barrier, inc=1, device_id=(x_partner(k),), device_id_type=MESH)
+
+    @pl.when(high_z == 0)
+    def _():
+        pl.semaphore_signal(barrier, inc=1, device_id=(across,), device_id_type=MESH)
+
+    for i in range(LOADS, GROUP):
+        load_px(i).start()
+        load_fl(i).start()
+
+    def enter():
+        pl.semaphore_wait(barrier, 15 + x + high_z)
+        for k in range(1, 4):
+            @pl.when(x + k >= 4)
+            def _():
+                pl.semaphore_signal(ready_far.at[0], inc=1, device_id=(x_partner(k),), device_id_type=MESH)
+
+        @pl.when(high_z == 1)
+        def _():
+            pl.semaphore_signal(ready_far.at[1], inc=1, device_id=(across,), device_id_type=MESH)
 
     my_rows = pl.multiple_of(pos * STRIP, STRIP)
 
     def piece(i):
         return pltpu.make_async_remote_copy(
             src_ref=send.at[i], dst_ref=out.at[pl.ds(my_rows, STRIP)],
-            send_sem=send_sem.at[i], recv_sem=recv_sem.at[i],
-            device_id=(base + partner(pos, i),), device_id_type=MESH)
-
-    def stat_copy(i):
+            send_sem=send_sem.at[i], recv_sem=recv_sem.at[pos],
+            device_id=(base + target(i),), device_id_type=MESH)
+
+    def arrived(source):
+        return pltpu.make_async_remote_copy(
+            src_ref=send.at[0], dst_ref=out.at[pl.ds(my_rows, STRIP)],
+            send_sem=send_sem.at[0], recv_sem=recv_sem.at[source],
+            device_id=(base + source,), device_id_type=MESH)
+
+    def stat_copy(code, slot):
         return pltpu.make_async_remote_copy(
             src_ref=stat.at[pos], dst_ref=stat.at[pos],
-            send_sem=s1_send.at[i], recv_sem=s1_recv.at[i],
-            device_id=(base + partner(pos, i),), device_id_type=MESH)
-
-    def total_copy(k):
-        other, there = far_partner(group, pos, k)
+            send_sem=s1_send.at[code], recv_sem=s1_recv.at[slot],
+            device_id=(base + moved(pos, code),), device_id_type=MESH)
+
+    def part_copy(k):
         return pltpu.make_async_remote_copy(
-            src_ref=total.at[group], dst_ref=total.at[group],
+            src_ref=part.at[x], dst_ref=part.at[x],
             send_sem=s2_send.at[k], recv_sem=s2_recv.at[k],
-            device_id=(other * GROUP + there,), device_id_type=MESH)
+            device_id=(x_partner(k),), device_id_type=MESH)
+
+    half_copy = pltpu.make_async_remote_copy(
+        src_ref=half.at[high_z], dst_ref=half.at[high_z], send_sem=s3_send, recv_sem=s3_recv,
+        device_id=(across,), device_id_type=MESH)
 
     lane = lax.broadcasted_iota(jnp.int32, (8, LANES), 1)
     row = lax.broadcasted_iota(jnp.int32, (8, LANES), 0)
@@ -155,13 +182,7 @@
 
         @pl.when(i == 0)
         def _():
-            pl.semaphore_wait(barrier, 15 + group)
-            for k in range(1, 8):
-                other, there = far_partner(group, pos, k)
-
-                @pl.when(other < group)
-                def _():
-                    pl.semaphore_signal(ready, inc=1, device_id=(other * GROUP + there,), device_id_type=MESH)
+            enter()
 
         @pl.when(i < EARLY)
         def _():
@@ -188,29 +209,39 @@
             stats = jnp.where((row == b) & (lane == s), value, stats)
     stat[pos] = stats
 
-    for i in range(15):
-        stat_copy(i).start()
+    for code in reversed(range(1, GROUP)):
+        stat_copy(code, pos).start()
     for i in range(EARLY, 15):
         piece(i).start()
 
-    for i in range(15):
-        stat_copy(i).wait_recv()
+    for code in range(1, GROUP):
+        stat_copy(code, moved(pos, code)).wait_recv()
     acc = stat[0]
     for k in range(1, GROUP):
         acc = merge(acc, stat[k], lane)
-    total[group] = acc
-    @pl.when(group < 7)
+    part[x] = acc
+
+    @pl.when(x < 3)
     def _():
-        pl.semaphore_wait(ready, 7 - group)
-
-    for k in range(1, 8):
-        total_copy(k).start()
-    for k in range(1, 8):
-        total_copy(k).wait_recv()
-
-    acc = total[0]
-    for k in range(1, 8):
-        acc = merge(acc, total[k], lane)
+        pl.semaphore_wait(ready_far.at[0], 3 - x)
+
+    for k in range(1, 4):
+        part_copy(k).start()
+    for k in range(1, 4):
+        part_copy(k).wait_recv()
+    acc = part[0]
+    for k in range(1, 4):
+        acc = merge(acc, part[k], lane)
+    half[high_z] = acc
+
+    @pl.when(high_z == 0)
+    def _():
+        pl.semaphore_wait(ready_far.at[1], 1)
+
+    half_copy.start()
+    half_copy.wait_recv()
+    acc = merge(half[0], half[1], lane)
+
     low, high, valid = acc[:, 0:1], acc[:, 1:2], acc[:, 2:3]
     divisor = jnp.maximum(valid, 1.0)
     average = acc[:, 3:4] / divisor
@@ -220,12 +251,14 @@
         lane == 2, valid / CELLS, jnp.where(lane == 3, average, deviation))))
     header[...] = table[:BANDS, :5]
 
-    for k in range(1, 8):
-        total_copy(k).wait_send()
+    half_copy.wait_send()
+    for k in range(1, 4):
+        part_copy(k).wait_send()
     for i in range(15):
-        stat_copy(i).wait_send()
         piece(i).wait_send()
-        piece(i).wait_recv()
+    for code in range(1, GROUP):
+        stat_copy(code, pos).wait_send()
+        arrived(moved(pos, code)).wait_recv()
 
 
 def place(tile, header, tile_out, header_out, sems):
@@ -242,12 +275,13 @@
 
 def on_device(pixels, valid_flags):
     dma = pltpu.SemaphoreType.DMA
+    shapes = (
+        jax.ShapeDtypeStruct((HALF, WIDE), jnp.float32),
+        jax.ShapeDtypeStruct((BANDS, 5), jnp.float32),
+    )
     tile, header = pl.pallas_call(
         kernel,
-        out_shape=(
-            jax.ShapeDtypeStruct((HALF, WIDE), jnp.float32),
-            jax.ShapeDtypeStruct((BANDS, 5), jnp.float32),
-        ),
+        out_shape=shapes,
         in_specs=[pl.BlockSpec(memory_space=pltpu.HBM)] * 2,
         out_specs=(pl.BlockSpec(memory_space=pltpu.VMEM), pl.BlockSpec(memory_space=pltpu.VMEM)),
         scratch_shapes=[
@@ -255,10 +289,11 @@
             pltpu.VMEM((GROUP, BANDS, STRIP, TILE), jnp.int32),
             pltpu.VMEM((GROUP - 1, STRIP, WIDE), jnp.float32),
             pltpu.VMEM((GROUP, 8, LANES), jnp.float32),
-            pltpu.VMEM((8, 8, LANES), jnp.float32),
-            dma((2, GROUP)), dma((GROUP - 1,)), dma((GROUP - 1,)),
-            dma((GROUP - 1,)), dma((GROUP - 1,)), dma((8,)), dma((8,)),
-            pltpu.SemaphoreType.REGULAR,
+            pltpu.VMEM((4, 8, LANES), jnp.float32),
+            pltpu.VMEM((2, 8, LANES), jnp.float32),
+            dma((2, GROUP)), dma((GROUP - 1,)), dma((GROUP,)),
+            dma((GROUP,)), dma((GROUP,)), dma((4,)), dma((4,)), dma, dma,
+            pltpu.SemaphoreType.REGULAR((2,)),
         ],
         compiler_params=pltpu.CompilerParams(
             collective_id=0, has_side_effects=True, vmem_limit_bytes=16 * 1024 * 1024),
@@ -269,10 +304,7 @@
     )
     tile, header = pl.pallas_call(
         place,
-        out_shape=(
-            jax.ShapeDtypeStruct((HALF, WIDE), jnp.float32),
-            jax.ShapeDtypeStruct((BANDS, 5), jnp.float32),
-        ),
+        out_shape=shapes,
         in_specs=[pl.BlockSpec(memory_space=pltpu.VMEM)] * 2,
         out_specs=(pl.BlockSpec(memory_space=pltpu.HBM), pl.BlockSpec(memory_space=pltpu.HBM)),
         scratch_shapes=[dma((PARTS + 1,))],

time: 35.3 us -> 34.5 us (0.977)
  the two profiles are of different devices: /device:TPU:6 before, /device:TPU:1 now
where the time goes in v6:
time: 34.5 us; the launch traced here: 34.4 us
  Pallas kernels  33.8 us (98%)
  between operations  0.64 us (2%)
    pallas_call x1, Pallas kernels, on_device(): pl.pallas_call(kernel, out_shape=shapes, in_specs=[pl.BlockSpec(memory_sp...  32.4 us
    pallas_call x1, Pallas kernels, on_device(): pl.pallas_call(place, out_shape=shapes, in_specs=[pl.BlockSpec(memory_spa...  1.36 us

profile of v6, /device:TPU:1, one launch (start us, length us, event | category | flops | bytes accessed | tf_op | source)
XLA Modules:
  0.0 34.4 jit_solution(13435993408696487171)
XLA Ops:
  0.6 32.4 %export.1 = (f32[256,2048]{1,0:T(8,128)S(1)}, f32[4,5]{1,0:T(4,128)S(1)}) custom-call(f32[4,16,8192]{2,1,0:T(8,128)} %px_hbm.1, s32[4,16,8192]{2,1,0:T(8,128)} %fl_hbm.1), custom_call_target="tpu_custom_call" | custom-call | tf_op jit(solution)/shard_map/export/pallas_call | solution.py:282
  33.1 1.4 %place.1 = (f32[256,2048]{1,0:T(8,128)}, f32[4,5]{1,0:T(4,128)}) custom-call(f32[256,2048]{1,0:T(8,128)S(1)} %get-tuple-element.6.tile, f32[4,5]{1,0:T(4,128)S(1)} %get-tuple-element.7.header), custom_call_target="tpu_custom_call" | custom-call | tf_op jit(solution)/shard_map/place/pallas_call | solution.py:305

commit v7 on v6

--- a/solution.py
+++ b/solution.py
@@ -20,18 +20,16 @@
 MESH = pl.DeviceIdType.MESH
 
 STEPS = (
-    (1, 2, 0), (0, 2, 0), (1, 2, 1), (0, 2, 1), (1, 1, 0), (0, 3, 0), (1, 3, 0), (0, 1, 0),
-    (1, 1, 1), (0, 3, 1), (1, 3, 1), (0, 1, 1), (1, 0, 0), (1, 0, 1), (0, 0, 1), (0, 0, 0),
+    (12, 2, 9, 13, 5, 10, 6, 14, 11, 7, 15, 3, 1, 4, 8, 0),
+    (2, 14, 4, 8, 9, 6, 11, 12, 1, 3, 5, 10, 13, 7, 15, 0),
 )
-NIBBLES = [z * 8 + y * 2 + c for z, y, c in STEPS]
-
 
 def packed(part):
     value = sum(code << (4 * k) for k, code in enumerate(part))
     return value - (1 << 32) if value >= 1 << 31 else value
 
 
-FIRST, SECOND = packed(NIBBLES[:8]), packed(NIBBLES[8:])
+WORDS = [(packed(steps[:8]), packed(steps[8:])) for steps in STEPS]
 
 
 def moved(pos, code):
@@ -49,7 +47,7 @@
     base = me - pos
     x = me >> 5
     high_z = (me >> 4) & 1
-    first, second = FIRST, SECOND
+    first, second = [jnp.where((me & 1) == 0, even, odd) for even, odd in zip(*WORDS)]
 
     def target(i):
         return moved(pos, (jnp.where(i < 8, first, second) >> ((i & 7) * 4)) & 15)

time: 34.5 us -> 33.5 us (0.971)
  the two profiles are of different devices: /device:TPU:1 before, /device:TPU:6 now
where the time goes in v7:
time: 33.5 us; the launch traced here: 33.2 us
  Pallas kernels  32.6 us (97%)
  between operations  0.64 us (2%)
    pallas_call x1, Pallas kernels, on_device(): pl.pallas_call(kernel, out_shape=shapes, in_specs=[pl.BlockSpec(memory_sp...  31.2 us
    pallas_call x1, Pallas kernels, on_device(): pl.pallas_call(place, out_shape=shapes, in_specs=[pl.BlockSpec(memory_spa...  1.36 us

profile of v7, /device:TPU:6, one launch (start us, length us, event | category | flops | bytes accessed | tf_op | source)
XLA Modules:
  0.0 33.2 jit_solution(35517858777005339)
XLA Ops:
  0.6 31.2 %export.1 = (f32[256,2048]{1,0:T(8,128)S(1)}, f32[4,5]{1,0:T(4,128)S(1)}) custom-call(f32[4,16,8192]{2,1,0:T(8,128)} %px_hbm.1, s32[4,16,8192]{2,1,0:T(8,128)} %fl_hbm.1), custom_call_target="tpu_custom_call" | custom-call | tf_op jit(solution)/shard_map/export/pallas_call | solution.py:280
  31.9 1.4 %place.1 = (f32[256,2048]{1,0:T(8,128)}, f32[4,5]{1,0:T(4,128)}) custom-call(f32[256,2048]{1,0:T(8,128)S(1)} %get-tuple-element.6.tile, f32[4,5]{1,0:T(4,128)S(1)} %get-tuple-element.7.header), custom_call_target="tpu_custom_call" | custom-call | tf_op jit(solution)/shard_map/place/pallas_call | solution.py:303

commit v8 on v7

--- a/solution.py
+++ b/solution.py
@@ -40,8 +40,8 @@
     return jnp.where(lane == 0, jnp.minimum(a, b), jnp.where(lane == 1, jnp.maximum(a, b), a + b))
 
 
-def kernel(px_hbm, fl_hbm, out, header, px, fl, send, stat, part, half, in_sem, send_sem, recv_sem,
-           s1_send, s1_recv, s2_send, s2_recv, s3_send, s3_recv, ready_far):
+def kernel(px_hbm, fl_hbm, out, header, px, fl, send, stat, part, half, in_sem, piece_sem, stat_sem,
+           part_sem, half_sem, ready_far):
     me = lax.axis_index("dev")
     pos = me & 15
     base = me - pos
@@ -59,11 +59,11 @@
 
     def load_px(i):
         at = pl.multiple_of(target(i) * TILE, TILE)
-        return pltpu.make_async_copy(px_hbm.at[:, :, pl.ds(at, TILE)], px.at[i], in_sem.at[0, i])
+        return pltpu.make_async_copy(px_hbm.at[:, :, pl.ds(at, TILE)], px.at[i], in_sem.at[i])
 
     def load_fl(i):
         at = pl.multiple_of(target(i) * TILE, TILE)
-        return pltpu.make_async_copy(fl_hbm.at[:, :, pl.ds(at, TILE)], fl.at[i], in_sem.at[1, i])
+        return pltpu.make_async_copy(fl_hbm.at[:, :, pl.ds(at, TILE)], fl.at[i], in_sem.at[i])
 
     barrier = pltpu.get_barrier_semaphore()
     for i in range(LOADS):
@@ -97,33 +97,23 @@
 
     my_rows = pl.multiple_of(pos * STRIP, STRIP)
 
+    def remote(src, dst, sems, there):
+        return pltpu.make_async_remote_copy(
+            src_ref=src, dst_ref=dst, send_sem=sems.at[0], recv_sem=sems.at[1], device_id=(there,), device_id_type=MESH)
+
     def piece(i):
-        return pltpu.make_async_remote_copy(
-            src_ref=send.at[i], dst_ref=out.at[pl.ds(my_rows, STRIP)],
-            send_sem=send_sem.at[i], recv_sem=recv_sem.at[pos],
-            device_id=(base + target(i),), device_id_type=MESH)
-
-    def arrived(source):
-        return pltpu.make_async_remote_copy(
-            src_ref=send.at[0], dst_ref=out.at[pl.ds(my_rows, STRIP)],
-            send_sem=send_sem.at[0], recv_sem=recv_sem.at[source],
-            device_id=(base + source,), device_id_type=MESH)
-
-    def stat_copy(code, slot):
-        return pltpu.make_async_remote_copy(
-            src_ref=stat.at[pos], dst_ref=stat.at[pos],
-            send_sem=s1_send.at[code], recv_sem=s1_recv.at[slot],
-            device_id=(base + moved(pos, code),), device_id_type=MESH)
+        return remote(send.at[i], out.at[pl.ds(my_rows, STRIP)], piece_sem, base + target(i))
+
+    def stat_copy(code):
+        return remote(stat.at[pos], stat.at[pos], stat_sem, base + moved(pos, code))
 
     def part_copy(k):
-        return pltpu.make_async_remote_copy(
-            src_ref=part.at[x], dst_ref=part.at[x],
-            send_sem=s2_send.at[k], recv_sem=s2_recv.at[k],
-            device_id=(x_partner(k),), device_id_type=MESH)
-
-    half_copy = pltpu.make_async_remote_copy(
-        src_ref=half.at[high_z], dst_ref=half.at[high_z], send_sem=s3_send, recv_sem=s3_recv,
-        device_id=(across,), device_id_type=MESH)
+        return remote(part.at[x], part.at[x], part_sem, x_partner(k))
+
+    all_pieces = remote(out.at[pl.ds(0, HALF - STRIP)], out.at[pl.ds(0, HALF - STRIP)], piece_sem, across)
+    all_stats = remote(stat.at[pl.ds(0, GROUP - 1)], stat.at[pl.ds(0, GROUP - 1)], stat_sem, across)
+    all_parts = remote(part.at[pl.ds(0, 3)], part.at[pl.ds(0, 3)], part_sem, across)
+    half_copy = remote(half.at[high_z], half.at[high_z], half_sem, across)
 
     lane = lax.broadcasted_iota(jnp.int32, (8, LANES), 1)
     row = lax.broadcasted_iota(jnp.int32, (8, LANES), 0)
@@ -131,8 +121,7 @@
     order = [((q + lane % 4) % 4) * 32 + lane // 4 for q in range(4)]
 
     def work(i, carry, store):
-        load_px(i).wait()
-        load_fl(i).wait()
+        pltpu.make_async_copy(px.at[pl.ds(0, 2)], px.at[pl.ds(0, 2)], in_sem.at[i]).wait()
         low, high, count, summed, square = [list(part) for part in carry]
         sums = [[] for _ in range(BANDS)]
         squares = [[] for _ in range(BANDS)]
@@ -208,12 +197,11 @@
     stat[pos] = stats
 
     for code in reversed(range(1, GROUP)):
-        stat_copy(code, pos).start()
+        stat_copy(code).start()
     for i in range(EARLY, 15):
         piece(i).start()
 
-    for code in range(1, GROUP):
-        stat_copy(code, moved(pos, code)).wait_recv()
+    all_stats.wait_recv()
     acc = stat[0]
     for k in range(1, GROUP):
         acc = merge(acc, stat[k], lane)
@@ -225,8 +213,7 @@
 
     for k in range(1, 4):
         part_copy(k).start()
-    for k in range(1, 4):
-        part_copy(k).wait_recv()
+    all_parts.wait_recv()
     acc = part[0]
     for k in range(1, 4):
         acc = merge(acc, part[k], lane)
@@ -250,13 +237,10 @@
     header[...] = table[:BANDS, :5]
 
     half_copy.wait_send()
-    for k in range(1, 4):
-        part_copy(k).wait_send()
-    for i in range(15):
-        piece(i).wait_send()
-    for code in range(1, GROUP):
-        stat_copy(code, pos).wait_send()
-        arrived(moved(pos, code)).wait_recv()
+    all_parts.wait_send()
+    all_stats.wait_send()
+    all_pieces.wait_send()
+    all_pieces.wait_recv()
 
 
 def place(tile, header, tile_out, header_out, sems):
@@ -289,8 +273,7 @@
             pltpu.VMEM((GROUP, 8, LANES), jnp.float32),
             pltpu.VMEM((4, 8, LANES), jnp.float32),
             pltpu.VMEM((2, 8, LANES), jnp.float32),
-            dma((2, GROUP)), dma((GROUP - 1,)), dma((GROUP,)),
-            dma((GROUP,)), dma((GROUP,)), dma((4,)), dma((4,)), dma, dma,
+            dma((GROUP,)), dma((2,)), dma((2,)), dma((2,)), dma((2,)),
             pltpu.SemaphoreType.REGULAR((2,)),
         ],
         compiler_params=pltpu.CompilerParams(

time: 33.5 us -> 32.7 us (0.976)
  Pallas kernels: 32.6 us -> 31.9 us
    pallas_call x1, Pallas kernels: 31.2 us -> 30.5 us  [on_device(): pl.pallas_call(kernel, out_shape=shapes, in_specs=[pl.BlockSpec(memory_sp...]
where the time goes in v8:
time: 32.7 us; the launch traced here: 32.5 us
  Pallas kernels  31.9 us (98%)
  between operations  0.64 us (2%)
    pallas_call x1, Pallas kernels, on_device(): pl.pallas_call(kernel, out_shape=shapes, in_specs=[pl.BlockSpec(memory_sp...  30.5 us
    pallas_call x1, Pallas kernels, on_device(): pl.pallas_call(place, out_shape=shapes, in_specs=[pl.BlockSpec(memory_spa...  1.36 us

profile of v8, /device:TPU:6, one launch (start us, length us, event | category | flops | bytes accessed | tf_op | source)
XLA Modules:
  0.0 32.5 jit_solution(7179300646792034247)
XLA Ops:
  0.6 30.5 %export.1 = (f32[256,2048]{1,0:T(8,128)S(1)}, f32[4,5]{1,0:T(4,128)S(1)}) custom-call(f32[4,16,8192]{2,1,0:T(8,128)} %px_hbm.1, s32[4,16,8192]{2,1,0:T(8,128)} %fl_hbm.1), custom_call_target="tpu_custom_call" | custom-call | tf_op jit(solution)/shard_map/export/pallas_call | solution.py:264
  31.1 1.4 %place.1 = (f32[256,2048]{1,0:T(8,128)}, f32[4,5]{1,0:T(4,128)}) custom-call(f32[256,2048]{1,0:T(8,128)S(1)} %get-tuple-element.6.tile, f32[4,5]{1,0:T(4,128)S(1)} %get-tuple-element.7.header), custom_call_target="tpu_custom_call" | custom-call | tf_op jit(solution)/shard_map/place/pallas_call | solution.py:286

commit v9 on v8

--- a/solution.py
+++ b/solution.py
@@ -14,8 +14,11 @@
 CELLS = 16777216.0
 LARGEST = 3e38
 LANES = 128
-EARLY = 2
+EARLIES = (6, 4)
+MIDDLE = 12
+SMALL = 7 + 3 + 1 + 1
 LOADS = 2
+GROUPS = (0, 1, 2, 4, 8)
 PARTS = 4
 MESH = pl.DeviceIdType.MESH
 
@@ -40,11 +43,13 @@
     return jnp.where(lane == 0, jnp.minimum(a, b), jnp.where(lane == 1, jnp.maximum(a, b), a + b))
 
 
-def kernel(px_hbm, fl_hbm, out, header, px, fl, send, stat, part, half, in_sem, piece_sem, stat_sem,
-           part_sem, half_sem, ready_far):
+def kernel(px_hbm, fl_hbm, out, header, px, fl, send, own, pair, stat, part, half, final, in_sem, piece_sem, small_sent, small_got,
+           ready_far):
     me = lax.axis_index("dev")
     pos = me & 15
     base = me - pos
+    core = me & 1
+    chip = pos >> 1
     x = me >> 5
     high_z = (me >> 4) & 1
     first, second = [jnp.where((me & 1) == 0, even, odd) for even, odd in zip(*WORDS)]
@@ -57,63 +62,64 @@
 
     across = me ^ 24
 
-    def load_px(i):
+    def start_load(i):
         at = pl.multiple_of(target(i) * TILE, TILE)
-        return pltpu.make_async_copy(px_hbm.at[:, :, pl.ds(at, TILE)], px.at[i], in_sem.at[i])
-
-    def load_fl(i):
-        at = pl.multiple_of(target(i) * TILE, TILE)
-        return pltpu.make_async_copy(fl_hbm.at[:, :, pl.ds(at, TILE)], fl.at[i], in_sem.at[i])
+        own = in_sem.at[max(g for g, start in enumerate(GROUPS) if start <= i)]
+        pltpu.make_async_copy(px_hbm.at[:, :, pl.ds(at, TILE)], px.at[i], own).start()
+        pltpu.make_async_copy(fl_hbm.at[:, :, pl.ds(at, TILE)], fl.at[i], own).start()
 
     barrier = pltpu.get_barrier_semaphore()
     for i in range(LOADS):
-        load_px(i).start()
-        load_fl(i).start()
+        start_load(i)
     for code in range(1, GROUP):
         pl.semaphore_signal(barrier, inc=1, device_id=(base + moved(pos, code),), device_id_type=MESH)
     for k in range(1, 4):
-        @pl.when(x + k < 4)
+        @pl.when((core == 1) & (x + k < 4))
         def _():
             pl.semaphore_signal(barrier, inc=1, device_id=(x_partner(k),), device_id_type=MESH)
 
-    @pl.when(high_z == 0)
+    @pl.when((core == 1) & (high_z == 0))
     def _():
         pl.semaphore_signal(barrier, inc=1, device_id=(across,), device_id_type=MESH)
 
     for i in range(LOADS, GROUP):
-        load_px(i).start()
-        load_fl(i).start()
+        start_load(i)
 
     def enter():
-        pl.semaphore_wait(barrier, 15 + x + high_z)
+        pl.semaphore_wait(barrier, 15 + core * (x + high_z))
         for k in range(1, 4):
-            @pl.when(x + k >= 4)
+            @pl.when((core == 1) & (x + k >= 4))
             def _():
                 pl.semaphore_signal(ready_far.at[0], inc=1, device_id=(x_partner(k),), device_id_type=MESH)
 
-        @pl.when(high_z == 1)
+        @pl.when((core == 1) & (high_z == 1))
         def _():
             pl.semaphore_signal(ready_far.at[1], inc=1, device_id=(across,), device_id_type=MESH)
 
     my_rows = pl.multiple_of(pos * STRIP, STRIP)
 
-    def remote(src, dst, sems, there):
+    def remote(src, dst, sent, got, there):
         return pltpu.make_async_remote_copy(
-            src_ref=src, dst_ref=dst, send_sem=sems.at[0], recv_sem=sems.at[1], device_id=(there,), device_id_type=MESH)
+            src_ref=src, dst_ref=dst, send_sem=sent, recv_sem=got, device_id=(there,), device_id_type=MESH)
 
     def piece(i):
-        return remote(send.at[i], out.at[pl.ds(my_rows, STRIP)], piece_sem, base + target(i))
+        return remote(send.at[i], out.at[pl.ds(my_rows, STRIP)], piece_sem.at[0], piece_sem.at[1],
+                      base + target(i))
 
     def stat_copy(code):
-        return remote(stat.at[pos], stat.at[pos], stat_sem, base + moved(pos, code))
+        return remote(stat.at[chip], stat.at[chip], small_sent, small_got.at[0], base + moved(pos, code))
 
     def part_copy(k):
-        return remote(part.at[x], part.at[x], part_sem, x_partner(k))
-
-    all_pieces = remote(out.at[pl.ds(0, HALF - STRIP)], out.at[pl.ds(0, HALF - STRIP)], piece_sem, across)
-    all_stats = remote(stat.at[pl.ds(0, GROUP - 1)], stat.at[pl.ds(0, GROUP - 1)], stat_sem, across)
-    all_parts = remote(part.at[pl.ds(0, 3)], part.at[pl.ds(0, 3)], part_sem, across)
-    half_copy = remote(half.at[high_z], half.at[high_z], half_sem, across)
+        return remote(part.at[x], part.at[x], small_sent, small_got.at[1], x_partner(k))
+
+    most = out.at[pl.ds(0, HALF - STRIP)]
+    all_pieces = remote(most, most, piece_sem.at[0], piece_sem.at[1], across)
+    all_stats = remote(stat.at[pl.ds(0, 7)], stat.at[pl.ds(0, 7)], small_sent, small_got.at[0], across)
+    all_parts = remote(part.at[pl.ds(0, 3)], part.at[pl.ds(0, 3)], small_sent, small_got.at[1], across)
+    half_copy = remote(half.at[high_z], half.at[high_z], small_sent, small_got.at[2], across)
+    pair_copy = remote(own, pair, small_sent, small_got.at[3], me ^ 1)
+    final_copy = remote(final, final, small_sent, small_got.at[3], me ^ 1)
+    all_small = remote(stat.at[pl.ds(0, SMALL)], stat.at[pl.ds(0, SMALL)], small_sent, small_got.at[0], across)
 
     lane = lax.broadcasted_iota(jnp.int32, (8, LANES), 1)
     row = lax.broadcasted_iota(jnp.int32, (8, LANES), 0)
@@ -121,7 +127,6 @@
     order = [((q + lane % 4) % 4) * 32 + lane // 4 for q in range(4)]
 
     def work(i, carry, store):
-        pltpu.make_async_copy(px.at[pl.ds(0, 2)], px.at[pl.ds(0, 2)], in_sem.at[i]).wait()
         low, high, count, summed, square = [list(part) for part in carry]
         sums = [[] for _ in range(BANDS)]
         squares = [[] for _ in range(BANDS)]
@@ -161,7 +166,16 @@
         (jnp.zeros((8, LANES), jnp.int32),) * BANDS, (zero,) * BANDS, (zero,) * BANDS,
     )
 
+    def wait_loads(g):
+        size = 2 * ((GROUPS + (GROUP,))[g + 1] - GROUPS[g])
+        pltpu.make_async_copy(px.at[pl.ds(0, size)], px.at[pl.ds(0, size)], in_sem.at[g]).wait()
+
     def step(i, carry):
+        for g, start in enumerate(GROUPS):
+            @pl.when(i == start)
+            def _():
+                wait_loads(g)
+
         def store(r, c, value):
             send[i, pl.ds(8 * r, 8), pl.ds(LANES * c, LANES)] = value
 
@@ -171,7 +185,7 @@
         def _():
             enter()
 
-        @pl.when(i < EARLY)
+        @pl.when(i < jnp.where(core == 0, EARLIES[0], EARLIES[1]))
         def _():
             piece(i).start()
 
@@ -194,39 +208,68 @@
             jnp.sum(square[b], axis=(0, 1), keepdims=True),
         )):
             stats = jnp.where((row == b) & (lane == s), value, stats)
-    stat[pos] = stats
-
-    for code in reversed(range(1, GROUP)):
-        stat_copy(code).start()
-    for i in range(EARLY, 15):
+    @pl.when(core == 0)
+    def _():
+        own[...] = stats
+        pair_copy.start()
+
+    @pl.when(core == 1)
+    def _():
+        pair_copy.wait_recv()
+        stat[chip] = merge(pair[...], stats, lane)
+        for code in range(14, 0, -2):
+            stat_copy(code).start()
+
+    @pl.when(core == 0)
+    def _():
+        for i in range(EARLIES[0], MIDDLE):
+            piece(i).start()
+
+    @pl.when(core == 1)
+    def _():
+        for i in range(EARLIES[1], MIDDLE):
+            piece(i).start()
+
+    @pl.when(core == 1)
+    def _():
+        all_stats.wait_recv()
+        acc = stat[0]
+        for k in range(1, 8):
+            acc = merge(acc, stat[k], lane)
+        part[x] = acc
+
+        @pl.when(x < 3)
+        def _():
+            pl.semaphore_wait(ready_far.at[0], 3 - x)
+
+        for k in range(1, 4):
+            part_copy(k).start()
+
+    for i in range(MIDDLE, 15):
         piece(i).start()
 
-    all_stats.wait_recv()
-    acc = stat[0]
-    for k in range(1, GROUP):
-        acc = merge(acc, stat[k], lane)
-    part[x] = acc
-
-    @pl.when(x < 3)
-    def _():
-        pl.semaphore_wait(ready_far.at[0], 3 - x)
-
-    for k in range(1, 4):
-        part_copy(k).start()
-    all_parts.wait_recv()
-    acc = part[0]
-    for k in range(1, 4):
-        acc = merge(acc, part[k], lane)
-    half[high_z] = acc
-
-    @pl.when(high_z == 0)
-    def _():
-        pl.semaphore_wait(ready_far.at[1], 1)
-
-    half_copy.start()
-    half_copy.wait_recv()
-    acc = merge(half[0], half[1], lane)
-
+    @pl.when(core == 1)
+    def _():
+        all_parts.wait_recv()
+        acc = part[0]
+        for k in range(1, 4):
+            acc = merge(acc, part[k], lane)
+        half[high_z] = acc
+
+        @pl.when(high_z == 0)
+        def _():
+            pl.semaphore_wait(ready_far.at[1], 1)
+
+        half_copy.start()
+        half_copy.wait_recv()
+        final[...] = merge(half[0], half[1], lane)
+        final_copy.start()
+
+    @pl.when(core == 0)
+    def _():
+        final_copy.wait_recv()
+
+    acc = final[...]
     low, high, valid = acc[:, 0:1], acc[:, 1:2], acc[:, 2:3]
     divisor = jnp.maximum(valid, 1.0)
     average = acc[:, 3:4] / divisor
@@ -236,9 +279,14 @@
         lane == 2, valid / CELLS, jnp.where(lane == 3, average, deviation))))
     header[...] = table[:BANDS, :5]
 
-    half_copy.wait_send()
-    all_parts.wait_send()
-    all_stats.wait_send()
+    @pl.when(core == 0)
+    def _():
+        pair_copy.wait_send()
+
+    @pl.when(core == 1)
+    def _():
+        all_small.wait_send()
+
     all_pieces.wait_send()
     all_pieces.wait_recv()
 
@@ -270,10 +318,13 @@
             pltpu.VMEM((GROUP, BANDS, STRIP, TILE), jnp.float32),
             pltpu.VMEM((GROUP, BANDS, STRIP, TILE), jnp.int32),
             pltpu.VMEM((GROUP - 1, STRIP, WIDE), jnp.float32),
-            pltpu.VMEM((GROUP, 8, LANES), jnp.float32),
+            pltpu.VMEM((8, LANES), jnp.float32),
+            pltpu.VMEM((8, LANES), jnp.float32),
+            pltpu.VMEM((SMALL, 8, LANES), jnp.float32),
             pltpu.VMEM((4, 8, LANES), jnp.float32),
             pltpu.VMEM((2, 8, LANES), jnp.float32),
-            dma((GROUP,)), dma((2,)), dma((2,)), dma((2,)), dma((2,)),
+            pltpu.VMEM((8, LANES), jnp.float32),
+            dma((len(GROUPS),)), dma((2,)), dma, dma((4,)),
             pltpu.SemaphoreType.REGULAR((2,)),
         ],
         compiler_params=pltpu.CompilerParams(

time: 32.7 us -> 32.1 us (0.982)
  Pallas kernels: 31.9 us -> 31.2 us
    pallas_call x1, Pallas kernels: 30.5 us -> 29.8 us  [on_device(): pl.pallas_call(kernel, out_shape=shapes, in_specs=[pl.BlockSpec(memory_sp...]
where the time goes in v9:
time: 32.1 us; the launch traced here: 31.8 us
  Pallas kernels  31.2 us (97%)
  between operations  0.64 us (2%)
    pallas_call x1, Pallas kernels, on_device(): pl.pallas_call(kernel, out_shape=shapes, in_specs=[pl.BlockSpec(memory_sp...  29.8 us
    pallas_call x1, Pallas kernels, on_device(): pl.pallas_call(place, out_shape=shapes, in_specs=[pl.BlockSpec(memory_spa...  1.36 us

profile of v9, /device:TPU:6, one launch (start us, length us, event | category | flops | bytes accessed | tf_op | source)
XLA Modules:
  0.0 31.8 jit_solution(8526899652408715967)
XLA Ops:
  0.6 29.8 %export.1 = (f32[256,2048]{1,0:T(8,128)S(1)}, f32[4,5]{1,0:T(4,128)S(1)}) custom-call(f32[4,16,8192]{2,1,0:T(8,128)} %px_hbm.1, s32[4,16,8192]{2,1,0:T(8,128)} %fl_hbm.1), custom_call_target="tpu_custom_call" | custom-call | tf_op jit(solution)/shard_map/export/pallas_call | solution.py:312
  30.5 1.4 %place.1 = (f32[256,2048]{1,0:T(8,128)}, f32[4,5]{1,0:T(4,128)}) custom-call(f32[256,2048]{1,0:T(8,128)S(1)} %get-tuple-element.6.tile, f32[4,5]{1,0:T(4,128)S(1)} %get-tuple-element.7.header), custom_call_target="tpu_custom_call" | custom-call | tf_op jit(solution)/shard_map/place/pallas_call | solution.py:337

commit v10 on v9

--- a/solution.py
+++ b/solution.py
@@ -23,8 +23,8 @@
 MESH = pl.DeviceIdType.MESH
 
 STEPS = (
-    (12, 2, 9, 13, 5, 10, 6, 14, 11, 7, 15, 3, 1, 4, 8, 0),
-    (2, 14, 4, 8, 9, 6, 11, 12, 1, 3, 5, 10, 13, 7, 15, 0),
+    (12, 9, 13, 5, 10, 6, 1, 11, 7, 15, 3, 14, 4, 8, 2, 0),
+    (2, 14, 8, 4, 9, 6, 11, 5, 12, 1, 3, 10, 13, 7, 15, 0),
 )
 
 def packed(part):

time: 32.1 us -> 31.8 us (level)
  no operation moved by 1% of the time
where the time goes in v10:
time: 31.8 us; the launch traced here: 31.5 us
  Pallas kernels  30.9 us (97%)
  between operations  0.64 us (2%)
    pallas_call x1, Pallas kernels, on_device(): pl.pallas_call(kernel, out_shape=shapes, in_specs=[pl.BlockSpec(memory_sp...  29.5 us
    pallas_call x1, Pallas kernels, on_device(): pl.pallas_call(place, out_shape=shapes, in_specs=[pl.BlockSpec(memory_spa...  1.36 us

profile of v10, /device:TPU:6, one launch (start us, length us, event | category | flops | bytes accessed | tf_op | source)
XLA Modules:
  0.0 31.5 jit_solution(7489120500442746002)
XLA Ops:
  0.6 29.5 %export.1 = (f32[256,2048]{1,0:T(8,128)S(1)}, f32[4,5]{1,0:T(4,128)S(1)}) custom-call(f32[4,16,8192]{2,1,0:T(8,128)} %px_hbm.1, s32[4,16,8192]{2,1,0:T(8,128)} %fl_hbm.1), custom_call_target="tpu_custom_call" | custom-call | tf_op jit(solution)/shard_map/export/pallas_call | solution.py:312
  30.2 1.4 %place.1 = (f32[256,2048]{1,0:T(8,128)}, f32[4,5]{1,0:T(4,128)}) custom-call(f32[256,2048]{1,0:T(8,128)S(1)} %get-tuple-element.6.tile, f32[4,5]{1,0:T(4,128)S(1)} %get-tuple-element.7.header), custom_call_target="tpu_custom_call" | custom-call | tf_op jit(solution)/shard_map/place/pallas_call | solution.py:337

commit v11 on v10

--- a/solution.py
+++ b/solution.py
@@ -14,7 +14,7 @@
 CELLS = 16777216.0
 LARGEST = 3e38
 LANES = 128
-EARLIES = (6, 4)
+EARLIES = (12, 4)
 MIDDLE = 12
 SMALL = 7 + 3 + 1 + 1
 LOADS = 2

time: 31.8 us -> 31.8 us (level)
  no operation moved by 1% of the time
where the time goes in v11:
time: 31.8 us; the launch traced here: 31.5 us
  Pallas kernels  30.9 us (97%)
  between operations  0.64 us (2%)
    pallas_call x1, Pallas kernels, on_device(): pl.pallas_call(kernel, out_shape=shapes, in_specs=[pl.BlockSpec(memory_sp...  29.5 us
    pallas_call x1, Pallas kernels, on_device(): pl.pallas_call(place, out_shape=shapes, in_specs=[pl.BlockSpec(memory_spa...  1.36 us

profile of v11, /device:TPU:6, one launch (start us, length us, event | category | flops | bytes accessed | tf_op | source)
XLA Modules:
  0.0 31.5 jit_solution(11150279660236565869)
XLA Ops:
  0.6 29.5 %export.1 = (f32[256,2048]{1,0:T(8,128)S(1)}, f32[4,5]{1,0:T(4,128)S(1)}) custom-call(f32[4,16,8192]{2,1,0:T(8,128)} %px_hbm.1, s32[4,16,8192]{2,1,0:T(8,128)} %fl_hbm.1), custom_call_target="tpu_custom_call" | custom-call | tf_op jit(solution)/shard_map/export/pallas_call | solution.py:312
  30.2 1.4 %place.1 = (f32[256,2048]{1,0:T(8,128)}, f32[4,5]{1,0:T(4,128)}) custom-call(f32[256,2048]{1,0:T(8,128)S(1)} %get-tuple-element.6.tile, f32[4,5]{1,0:T(4,128)S(1)} %get-tuple-element.7.header), custom_call_target="tpu_custom_call" | custom-call | tf_op jit(solution)/shard_map/place/pallas_call | solution.py:337

commit v12 on v10

--- a/solution.py
+++ b/solution.py
@@ -23,8 +23,8 @@
 MESH = pl.DeviceIdType.MESH
 
 STEPS = (
-    (12, 9, 13, 5, 10, 6, 1, 11, 7, 15, 3, 14, 4, 8, 2, 0),
-    (2, 14, 8, 4, 9, 6, 11, 5, 12, 1, 3, 10, 13, 7, 15, 0),
+    (12, 13, 9, 5, 11, 6, 1, 10, 7, 15, 14, 3, 4, 8, 2, 0),
+    (2, 14, 4, 8, 9, 6, 11, 5, 15, 12, 1, 3, 10, 13, 7, 0),
 )
 
 def packed(part):

time: 31.8 us -> 31.8 us (level)
  no operation moved by 1% of the time
where the time goes in v12:
time: 31.8 us; the launch traced here: 31.5 us
  Pallas kernels  30.9 us (97%)
  between operations  0.64 us (2%)
    pallas_call x1, Pallas kernels, on_device(): pl.pallas_call(kernel, out_shape=shapes, in_specs=[pl.BlockSpec(memory_sp...  29.5 us
    pallas_call x1, Pallas kernels, on_device(): pl.pallas_call(place, out_shape=shapes, in_specs=[pl.BlockSpec(memory_spa...  1.36 us

profile of v12, /device:TPU:6, one launch (start us, length us, event | category | flops | bytes accessed | tf_op | source)
XLA Modules:
  0.0 31.5 jit_solution(267132906097365385)
XLA Ops:
  0.6 29.5 %export.1 = (f32[256,2048]{1,0:T(8,128)S(1)}, f32[4,5]{1,0:T(4,128)S(1)}) custom-call(f32[4,16,8192]{2,1,0:T(8,128)} %px_hbm.1, s32[4,16,8192]{2,1,0:T(8,128)} %fl_hbm.1), custom_call_target="tpu_custom_call" | custom-call | tf_op jit(solution)/shard_map/export/pallas_call | solution.py:312
  30.2 1.4 %place.1 = (f32[256,2048]{1,0:T(8,128)}, f32[4,5]{1,0:T(4,128)}) custom-call(f32[256,2048]{1,0:T(8,128)S(1)} %get-tuple-element.6.tile, f32[4,5]{1,0:T(4,128)S(1)} %get-tuple-element.7.header), custom_call_target="tpu_custom_call" | custom-call | tf_op jit(solution)/shard_map/place/pallas_call | solution.py:337
